TPU v7x, 16 devices: a 4x2x1 block of a 4x4x8 slice. The times are simulated.
16 devices in a mesh: dp: 2 (over y, z), tp: 8 (over x, core).
Axes of the slice: x: 4, y: 2, z: 1, core: 2. Of those that a mesh axis runs over, the one named last changes fastest.
The devices are a block of a 4x4x8 slice.
Arguments:
- hidden: bfloat16 [6, 1536, 2048], P('dp', 'tp'), parts along dimension 0
- grad_out: bfloat16 [6, 1536, 2048], P('dp', 'tp'), parts along dimension 0
- prefix_len: int32 [6], P('dp'), parts along dimension 0
- valid_len: int32 [6], P('dp'), parts along dimension 0
- attn_norm: bfloat16 [2048], replicated
- w_query: bfloat16 [2048, 2048], P(None, 'tp')
- w_key: bfloat16 [2048, 256], replicated
- w_value: bfloat16 [2048, 256], replicated
- w_out: bfloat16 [2048, 2048], P('tp')
- mlp_norm: bfloat16 [2048], replicated
- w_gate: bfloat16 [2048, 16384], P(None, 'tp')
- w_up: bfloat16 [2048, 16384], P(None, 'tp')
- w_down: bfloat16 [16384, 2048], P('tp')
Outputs:
- output 1: bfloat16 [6, 1536, 2048], P('dp', 'tp'), parts along dimension 0
- output 2: bfloat16 [6, 1536, 2048], P('dp', 'tp'), parts along dimension 0
- output 3: float32 [4096], P('dp'), parts along dimension 0
- output 4: float32 [4096, 2048], P('dp', 'tp'), parts along dimension 0
- output 5: float32 [4096, 256], P('dp'), parts along dimension 0
- output 6: float32 [4096, 256], P('dp'), parts along dimension 0
- output 7: float32 [4096, 2048], P(('dp', 'tp')), parts along dimension 0
- output 8: float32 [4096], P('dp'), parts along dimension 0
- output 9: float32 [4096, 16384], P('dp', 'tp'), parts along dimension 0
- output 10: float32 [4096, 16384], P('dp', 'tp'), parts along dimension 0
- output 11: float32 [32768, 2048], P(('dp', 'tp')), parts along dimension 0
There are 2 independent parts. A program takes and returns all parts, laid end to end along the dimension named above; an argument that names none is the same for every part.
All inputs are finite; a program needn't handle non-finite values.
Results may differ from a plain program's by a relative error of at most 0.02.
Values are sent between devices in bfloat16 or wider.
A program may use at most 768 MiB of HBM per device.

v0:
```python
import math
import jax
import jax.numpy as jnp
from jax import lax
from jax.sharding import PartitionSpec as P

NORM_EPS = 1e-6


def rms_norm(x_in, gain):
    x_f = x_in.astype(jnp.float32)
    inv_rms = lax.rsqrt(jnp.mean(x_f * x_f, axis=-1, keepdims=True) + NORM_EPS)
    return (x_f * inv_rms * (1.0 + gain)).astype(jnp.bfloat16)


def rope_tables(positions, head_dim):
    half_dim = head_dim // 2
    exponent = jnp.arange(half_dim, dtype=jnp.float32) * (2.0 / head_dim)
    inv_freq = jnp.exp(exponent * (-math.log(10000.0)))
    angles = positions.astype(jnp.float32)[:, None] * inv_freq[None, :]
    return jnp.cos(angles), jnp.sin(angles)


def apply_rope(x_f, cos_t, sin_t):
    half_dim = x_f.shape[-1] // 2
    first = x_f[..., :half_dim]
    second = x_f[..., half_dim:]
    return jnp.concatenate([first * cos_t - second * sin_t, second * cos_t + first * sin_t], axis=-1)


def attend(query, keys, values, prefix_len, valid_len, first_pos):
    scale = query.shape[-1] ** -0.5
    scores = jnp.einsum("crie,cle->cirl", query, keys, preferred_element_type=jnp.float32) * scale
    q_pos = first_pos + jnp.arange(query.shape[1])
    k_pos = jnp.arange(keys.shape[1])
    key_row = k_pos[None, None, :]
    visible = (key_row < valid_len[:, None, None]) & ((key_row < prefix_len[:, None, None]) | (key_row <= q_pos[None, :, None]))
    scores = jnp.where(visible[:, None, :, :], scores, -1e30)
    probs = jax.nn.softmax(scores, axis=-1).astype(jnp.bfloat16)
    return jnp.einsum("cirl,cle->crie", probs, values, preferred_element_type=jnp.float32).astype(jnp.bfloat16)


def gated_act(gate, upper):
    return (jax.nn.gelu(gate, approximate=True) * upper).astype(jnp.bfloat16)


def gather_seq(x_loc):
    return lax.all_gather(x_loc, "tp", axis=1, tiled=True)


def scatter_seq(x_part):
    return lax.psum_scatter(x_part, "tp", scatter_dimension=1, tiled=True)


def solution(mesh):
    tp_size = mesh.shape["tp"]
    act_spec = P("dp", "tp", None)
    in_specs = (act_spec, act_spec, P("dp"), P("dp"), P(None), P(None, "tp"), P(None, None), P(None, None), P("tp", None), P(None), P(None, "tp"), P(None, "tp"), P("tp", None))
    out_specs = (act_spec, act_spec, P("dp"), P("dp", "tp"), P("dp", None), P("dp", None), P(("dp", "tp"), None), P("dp"), P("dp", "tp"), P("dp", "tp"), P(("dp", "tp"), None))

    def local_layer(hidden, grad_out, prefix_len, valid_len, attn_norm, w_query, w_key, w_value, w_out, mlp_norm, w_gate, w_up, w_down):
        batch, shard_len, model_dim = hidden.shape
        head_dim = w_key.shape[1]
        local_heads = w_query.shape[1] // head_dim
        seq_len = shard_len * tp_size
        cos_t, sin_t = rope_tables(jnp.arange(seq_len), head_dim)

        def rope_heads(raw_proj):
            return apply_rope(raw_proj, cos_t[:, None, :], sin_t[:, None, :]).astype(jnp.bfloat16)

        def rope_single(raw_proj):
            return apply_rope(raw_proj, cos_t, sin_t).astype(jnp.bfloat16)

        def attend_here(q_in, k_in, v_in):
            return attend(q_in, k_in, v_in, prefix_len, valid_len, 0)

        normed, norm1_pull = jax.vjp(rms_norm, hidden, attn_norm.astype(jnp.float32))
        normed_all = gather_seq(normed)
        q_raw = jnp.einsum("bld,dn->bln", normed_all, w_query, preferred_element_type=jnp.float32).reshape(batch, seq_len, local_heads, head_dim)
        query, query_pull = jax.vjp(rope_heads, q_raw)
        k_raw = jnp.einsum("bld,de->ble", normed_all, w_key, preferred_element_type=jnp.float32)
        keys, key_pull = jax.vjp(rope_single, k_raw)
        values = jnp.einsum("bld,de->ble", normed_all, w_value, preferred_element_type=jnp.float32).astype(jnp.bfloat16)
        mixed, attn_pull = jax.vjp(attend_here, query, keys, values)
        w_out_heads = w_out.reshape(local_heads, head_dim, model_dim)
        attn_part = jnp.einsum("blhd,hde->ble", mixed, w_out_heads, preferred_element_type=jnp.float32).astype(jnp.bfloat16)
        attn_sum = scatter_seq(attn_part)
        resid = (hidden.astype(jnp.float32) + attn_sum.astype(jnp.float32)).astype(jnp.bfloat16)
        gated_in, norm2_pull = jax.vjp(rms_norm, resid, mlp_norm.astype(jnp.float32))
        gated_all = gather_seq(gated_in)
        gate = jnp.einsum("bld,df->blf", gated_all, w_gate, preferred_element_type=jnp.float32)
        upper = jnp.einsum("bld,df->blf", gated_all, w_up, preferred_element_type=jnp.float32)
        act, act_pull = jax.vjp(gated_act, gate, upper)
        mlp_part = jnp.einsum("blf,fd->bld", act, w_down, preferred_element_type=jnp.float32).astype(jnp.bfloat16)
        mlp_sum = scatter_seq(mlp_part)
        hidden_out = (resid.astype(jnp.float32) + mlp_sum.astype(jnp.float32)).astype(jnp.bfloat16)

        grad_all = gather_seq(grad_out)
        g_down = jnp.einsum("blf,bld->fd", act, grad_all, preferred_element_type=jnp.float32)
        d_act = jnp.einsum("bld,fd->blf", grad_all, w_down, preferred_element_type=jnp.float32).astype(jnp.bfloat16)
        d_gate, d_upper = act_pull(d_act)
        d_gate = d_gate.astype(jnp.bfloat16)
        d_upper = d_upper.astype(jnp.bfloat16)
        g_gate = jnp.einsum("bld,blf->df", gated_all, d_gate, preferred_element_type=jnp.float32)
        g_up = jnp.einsum("bld,blf->df", gated_all, d_upper, preferred_element_type=jnp.float32)
        d_gated_part = (jnp.einsum("blf,df->bld", d_gate, w_gate, preferred_element_type=jnp.float32)
                        + jnp.einsum("blf,df->bld", d_upper, w_up, preferred_element_type=jnp.float32)).astype(jnp.bfloat16)
        d_gated = scatter_seq(d_gated_part)
        d_resid_norm, g_mlp_norm_part = norm2_pull(d_gated)
        g_mlp_norm = lax.psum(g_mlp_norm_part, "tp")
        d_resid = (grad_out.astype(jnp.float32) + d_resid_norm.astype(jnp.float32)).astype(jnp.bfloat16)

        d_resid_all = gather_seq(d_resid)
        g_out = jnp.einsum("blhd,ble->hde", mixed, d_resid_all, preferred_element_type=jnp.float32).reshape(local_heads * head_dim, model_dim)
        d_mixed = jnp.einsum("ble,hde->blhd", d_resid_all, w_out_heads, preferred_element_type=jnp.float32).astype(jnp.bfloat16)
        d_query, d_keys, d_values = attn_pull(d_mixed)
        d_q_raw = query_pull(d_query)[0].astype(jnp.bfloat16).reshape(batch, seq_len, local_heads * head_dim)
        d_k_raw = key_pull(d_keys)[0].astype(jnp.bfloat16)
        g_query = jnp.einsum("bld,bln->dn", normed_all, d_q_raw, preferred_element_type=jnp.float32)
        g_key = lax.psum(jnp.einsum("bld,ble->de", normed_all, d_k_raw, preferred_element_type=jnp.float32), "tp")
        g_value = lax.psum(jnp.einsum("bld,ble->de", normed_all, d_values, preferred_element_type=jnp.float32), "tp")
        d_normed_part = (jnp.einsum("bln,dn->bld", d_q_raw, w_query, preferred_element_type=jnp.float32)
                         + jnp.einsum("ble,de->bld", d_k_raw, w_key, preferred_element_type=jnp.float32)
                         + jnp.einsum("ble,de->bld", d_values, w_value, preferred_element_type=jnp.float32)).astype(jnp.bfloat16)
        d_normed = scatter_seq(d_normed_part)
        d_hidden_norm, g_attn_norm_part = norm1_pull(d_normed)
        g_attn_norm = lax.psum(g_attn_norm_part, "tp")
        grad_hidden = (d_resid.astype(jnp.float32) + d_hidden_norm.astype(jnp.float32)).astype(jnp.bfloat16)
        return (hidden_out, grad_hidden, g_attn_norm, g_query, g_key, g_value, g_out, g_mlp_norm, g_gate, g_up, g_down)

    return jax.shard_map(local_layer, mesh=mesh, in_specs=in_specs, out_specs=out_specs, check_vma=False)
```

profile of v0, /device:TPU:112, one launch (start us, length us, event | category | flops | bytes accessed | tf_op | source)
XLA Modules:
  0.0 1417.2 jit_solution(3903159712743589021)
XLA Ops:
  7.3 2.3 fusion.45
  9.6 0.6 copy-done.37
  10.2 0.7 convert_add_fusion.3
  10.9 0.6 copy-done.27
  11.5 3.7 fusion.40
  15.4 2.8 multiply_cosine_fusion
  18.3 2.1 iota_compare_fusion
  20.3 87.9 %all-gather.5.cloned.1.call-done = bf16[3,1536,2048]{2,1,0:T(8,128)(2,1)} async-done(((bf16[3,192,2048]{2,1,0:T(8,128)(2,1)}), bf16[3,1536,2048]{2,1,0:T(8,128)(2,1)}) %all-gather.5.cloned.1.call-update) | async-done | bytes 18874384 | tf_op jit(solution)/shard_map/all_gather | solution.py:48
  108.2 9.6 convolution_bitcast_fusion.3
  117.9 2.3 fusion.78
  120.1 9.5 fusion.87
  129.7 0.9 subtract_convert_fusion.1
  130.6 0.7 copy-done.9
  131.3 0.6 copy-done.24
  131.9 0.9 copy-done.25
  132.8 12.7 fusion.17
  145.5 14.7 %fusion.106 = f32[3,1536]{1,0:T(4,128)S(1)} fusion(f32[3,1536]{1,0:T(4,128)S(1)} %get-tuple-element.35, f32[3,1536,1536]{2,1,0:T(8,128)} %get-tuple-element.36, pred[1536,1536]{0,1:T(8,128)(4,1)S(1)} %copy-done.9, pred[3,1536]{1,0:T(4,128)(4,1)S(1)} %get-tuple-element.40, pred[3,1536]{1,0:T(4,128)(4,1)S(1)} %get-tuple-element.41), kind=kLoop, calls=%fused_computation.158 | loop fusion | flops 42462720 | bytes 30716928 | tf_op jit(solution)/shard_map/jvp()/reduce_sum | solution.py:39
  160.2 9.4 convolution_convert_fusion.5
  169.7 16.3 %fusion.66 = bf16[3,1536,256]{1,2,0:T(8,128)(2,1)S(1)} fusion(bf16[3,1536,256]{2,1,0:T(8,128)(2,1)S(1)} %convolution_convert_fusion.5, f32[3,1536]{1,0:T(4,128)S(1)} %fusion.106, f32[3,1536]{1,0:T(4,128)S(1)} %get-tuple-element.35, f32[3,1536,1536]{2,1,0:T(8,128)} %get-tuple-element.36, pred[1536,1536]{0,1:T(8,128)(4,1)S(1)} %copy-done.9, ...), kind=kOutput, calls=%fused_computation.99 | convolution fusion | flops 3674603520 | bytes 35435520 | tf_op jit(solution)/shard_map/jvp(cirl,cle->crie)/dot_general | solution.py:40
  186.1 1.4 copy-done.20
  187.5 9.2 convolution_convert_fusion.3
  196.9 0.7 all-gather.9.cloned.1.call-update
  197.7 97.5 %reduce-scatter.5.cloned.1.call-done = bf16[3,192,2048]{2,1,0:T(8,128)(2,1)} async-done(((bf16[3,1536,2048]{2,1,0:T(8,128)(2,1)}), bf16[3,192,2048]{2,1,0:T(8,128)(2,1)}) %reduce-scatter.5.cloned.1.call-update) | async-done | bytes 2359312 | tf_op jit(solution)/shard_map/reduce_scatter | solution.py:52
  295.2 2.6 fusion.48
  298.4 0.8 copy-done.3
  299.2 2.0 fusion.39
  301.4 85.1 %all-gather.9.cloned.1.call-done = bf16[3,1536,2048]{2,1,0:T(8,128)(2,1)} async-done(((bf16[3,192,2048]{2,1,0:T(8,128)(2,1)}), bf16[3,1536,2048]{2,1,0:T(8,128)(2,1)}) %all-gather.9.cloned.1.call-update) | async-done | bytes 18874384 | tf_op jit(solution)/shard_map/all_gather | solution.py:48
  386.5 46.6 %convolution_convert_fusion.1 = bf16[3,1536,2048]{2,1,0:T(8,128)(2,1)} fusion(bf16[3,1536,2048]{2,1,0:T(8,128)(2,1)} %all-gather.9.cloned.1.call-done, bf16[2048,2048]{1,0:T(8,128)(2,1)} %param.25), kind=kOutput, calls=%fused_computation.37 | convolution fusion | flops 38664142848 | bytes 46137344 | tf_op jit(solution)/shard_map/bld,fd->blf/dot_general | solution.py:100
  433.1 46.1 %all-gather.7.cloned.1.call-done = bf16[3,1536,2048]{2,1,0:T(8,128)(2,1)} async-done(((bf16[3,192,2048]{2,1,0:T(8,128)(2,1)}), bf16[3,1536,2048]{2,1,0:T(8,128)(2,1)}) %all-gather.7.cloned.1.call-update) | async-done | bytes 18874384 | tf_op jit(solution)/shard_map/all_gather | solution.py:48
  479.2 47.0 %fusion.25 = f32[3,1536,2048]{2,1,0:T(8,128)} fusion(bf16[3,1536,2048]{2,1,0:T(8,128)(2,1)} %all-gather.7.cloned.1.call-done, bf16[2048,2048]{1,0:T(8,128)(2,1)} %param.24), kind=kOutput, calls=%fused_computation.57 | convolution fusion | flops 38654705664 | bytes 65011712 | tf_op jit(solution)/shard_map/bld,df->blf/dot_general | solution.py:92
  526.2 77.4 %fusion.7 = (bf16[3,1536,2048]{2,1,0:T(8,128)(2,1)}, bf16[3,1536,2048]{2,1,0:T(8,128)(2,1)}, f32[3,1536,2048]{2,1,0:T(8,128)}) fusion(f32[3,1536,2048]{2,1,0:T(8,128)} %fusion.25, bf16[3,1536,2048]{2,1,0:T(8,128)(2,1)} %convolution_convert_fusion.1, bf16[3,1536,2048]{2,1,0:T(8,128)(2,1)} %all-gather.7.cloned.1.call-done, bf16[2048,2048]{1,0:T(8,128)(2,1)} %param.23), kind=kOutput, calls=%fused_computation.11 | convolution fusion | flops 38890635264 | bytes 159383552 | tf_op jit(solution)/shard_map/bld,df->blf/dot_general | solution.py:91
  603.6 47.5 %fusion.27 = f32[3,1536,2048]{2,1,0:T(8,128)} fusion(bf16[3,1536,2048]{2,1,0:T(8,128)(2,1)} %get-tuple-element.21, bf16[2048,2048]{1,0:T(8,128)(2,1)} %param.23), kind=kOutput, calls=%fused_computation.59 | convolution fusion | flops 38654705664 | bytes 65011712 | tf_op jit(solution)/shard_map/blf,df->bld/dot_general | solution.py:106
  651.1 54.3 %add_convert_fusion.1 = bf16[3,1536,2048]{2,1,0:T(8,128)(2,1)} fusion(f32[3,1536,2048]{2,1,0:T(8,128)} %fusion.27, bf16[2048,2048]{1,0:T(8,128)(2,1)} %param.24, bf16[3,1536,2048]{2,1,0:T(8,128)(2,1)} %convolution_convert_fusion.1, f32[3,1536,2048]{2,1,0:T(8,128)} %get-tuple-element.37), kind=kOutput, calls=%fused_computation.13 | convolution fusion | flops 38777389056 | bytes 121634816 | tf_op jit(solution)/shard_map/blf,df->bld/dot_general | solution.py:107
  705.5 46.4 %convolution_convert_fusion.2 = bf16[3,1536,2048]{2,1,0:T(8,128)(2,1)} fusion(bf16[3,1536,2048]{2,1,0:T(8,128)(2,1)} %get-tuple-element.22, bf16[2048,2048]{1,0:T(8,128)(2,1)} %param.25), kind=kOutput, calls=%fused_computation.38 | convolution fusion | flops 38664142848 | bytes 46137344 | tf_op jit(solution)/shard_map/blf,fd->bld/dot_general | solution.py:94
  752.1 51.8 %reduce-scatter.9.cloned.1.call-done = bf16[3,192,2048]{2,1,0:T(8,128)(2,1)} async-done(((bf16[3,1536,2048]{2,1,0:T(8,128)(2,1)}), bf16[3,192,2048]{2,1,0:T(8,128)(2,1)}) %reduce-scatter.9.cloned.1.call-update) | async-done | bytes 2359312 | tf_op jit(solution)/shard_map/reduce_scatter | solution.py:52
  803.8 4.3 fusion.41
  808.2 95.2 %reduce-scatter.7.cloned.1.call-done = bf16[3,192,2048]{2,1,0:T(8,128)(2,1)} async-done(((bf16[3,1536,2048]{2,1,0:T(8,128)(2,1)}), bf16[3,192,2048]{2,1,0:T(8,128)(2,1)}) %reduce-scatter.7.cloned.1.call-update) | async-done | bytes 2359312 | tf_op jit(solution)/shard_map/reduce_scatter | solution.py:52
  903.3 6.1 add_convert_fusion.5
  909.6 89.7 %all-gather.11.cloned.1.call-done = bf16[3,1536,2048]{2,1,0:T(8,128)(2,1)} async-done(((bf16[3,192,2048]{2,1,0:T(8,128)(2,1)}), bf16[3,1536,2048]{2,1,0:T(8,128)(2,1)}) %all-gather.11.cloned.1.call-update) | async-done | bytes 18874384 | tf_op jit(solution)/shard_map/all_gather | solution.py:48
  999.3 9.4 fusion.75
  1008.7 1.4 copy-done.52
  1010.1 16.3 %fusion.63 = bf16[3,1536,256]{2,1,0:T(8,128)(2,1)} fusion(bf16[3,256,1536]{1,2,0:T(8,128)(2,1)S(1)} %fusion.75, f32[3,1536]{1,0:T(4,128)S(1)} %copy-done.32, f32[3,1536]{1,0:T(4,128)S(1)} %copy-done.43, f32[3,1536,1536]{2,1,0:T(8,128)} %get-tuple-element.36, pred[1536,1536]{0,1:T(8,128)(4,1)S(1)} %copy-done.10, pred[3,1536]{1,0:T(4,128)(4,1)S(1)} %copy-done.45, ...), kind=kOutput, calls=%fused_computation.98 | convolution fusion | flops 3674603520 | bytes 35435520 | tf_op jit(solution)/shard_map/transpose(jvp(cirl,cle->crie))/dot_general | solution.py:40
  1026.4 22.0 %fusion.16 = (f32[3,1536]{1,0:T(4,128)S(1)}, bf16[3,1536,1536]{1,2,0:T(8,128)(2,1)}) fusion(f32[3,1536]{1,0:T(4,128)S(1)} %multiply_divide_fusion, f32[3,1536]{1,0:T(4,128)S(1)} %copy-done.43, f32[3,1536,1536]{2,1,0:T(8,128)} %get-tuple-element.36, pred[1536,1536]{0,1:T(8,128)(4,1)S(1)} %copy-done.10, pred[3,1536]{1,0:T(4,128)(4,1)S(1)} %copy-done.45, ...), kind=kOutput, calls=%fused_computation.26 | convolution fusion | flops 3694652928 | bytes 49609728 | tf_op jit(solution)/shard_map/transpose(jvp(cirl,cle->crie))/dot_general | solution.py:40
  1048.4 23.1 %fusion.57 = f32[3,1536,256]{1,2,0:T(8,128)} fusion(bf16[3,1536,1536]{1,2,0:T(8,128)(2,1)} %get-tuple-element.39, f32[3,1536]{1,0:T(4,128)S(1)} %neg.13, f32[3,1536]{1,0:T(4,128)S(1)} %copy-done.32, pred[1536,1536]{0,1:T(8,128)(4,1)S(1)} %copy-done.10, pred[3,1536]{1,0:T(4,128)(4,1)S(1)} %copy-done.45, pred[3,1536]{1,0:T(4,128)(4,1)S(1)} %copy-done.47, ...), kind=kOutput, calls=%fused_computation.96 | convolution fusion | flops 3708813312 | bytes 51969024 | tf_op jit(solution)/shard_map/transpose(jvp(crie,cle->cirl))/dot_general | solution.py:33
  1071.6 21.0 %fusion.72 = f32[3,1536,1,256]{1,3,0,2:T(8,128)S(1)} fusion(bf16[3,1536,1536]{1,2,0:T(8,128)(2,1)} %get-tuple-element.39, f32[3,1536]{1,0:T(4,128)S(1)} %neg.13, f32[3,1536]{1,0:T(4,128)S(1)} %copy-done.32, pred[1536,1536]{0,1:T(8,128)(4,1)S(1)} %copy-done.10, pred[3,1536]{1,0:T(4,128)(4,1)S(1)} %copy-done.45, pred[3,1536]{1,0:T(4,128)(4,1)S(1)} %copy-done.47, ...), kind=kOutput, calls=%fused_computation.101 | convolution fusion | flops 3708813312 | bytes 51969024 | tf_op jit(solution)/shard_map/transpose(jvp(crie,cle->cirl))/dot_general | solution.py:33
  1092.6 0.7 multiply_add_fusion.3
  1093.4 1.6 copy-done.17
  1094.9 2.5 multiply_add_fusion.1
  1097.5 17.2 %fusion.85 = f32[3,1536,2048]{2,1,0:T(8,128)} fusion(bf16[2048,256]{1,0:T(8,128)(2,1)} %param.19, f32[3,1536,128]{1,2,0:T(8,128)} %get-tuple-element.24, f32[3,1536,128]{1,2,0:T(8,128)S(1)} %get-tuple-element.23), kind=kOutput, calls=%fused_computation.128 | convolution fusion | flops 4834197504 | bytes 43515904 | tf_op jit(solution)/shard_map/ble,de->bld/dot_general | solution.py:123
  1114.7 16.2 %fusion.82 = f32[3,1536,2048]{2,1,0:T(8,128)} fusion(bf16[2048,256]{1,0:T(8,128)(2,1)} %param.18, f32[3,1536,1,128]{1,3,0,2:T(8,128)S(1)} %get-tuple-element.26, f32[3,1536,1,128]{1,3,0,2:T(8,128)S(1)} %get-tuple-element.25), kind=kOutput, calls=%fused_computation.125 | convolution fusion | flops 4834197504 | bytes 43515904 | tf_op jit(solution)/shard_map/bln,dn->bld/dot_general | solution.py:122
  1130.9 31.7 %add_convert_fusion = bf16[3,1536,2048]{2,1,0:T(8,128)(2,1)} fusion(f32[3,1536,2048]{2,1,0:T(8,128)} %fusion.82, f32[3,1536,2048]{2,1,0:T(8,128)} %fusion.85, bf16[3,1536,256]{2,1,0:T(8,128)(2,1)S(1)} %copy-done.18, bf16[2048,256]{1,0:T(8,128)(2,1)} %param.20), kind=kOutput, calls=%fused_computation.12 | convolution fusion | flops 4860149760 | bytes 97779712 | tf_op jit(solution)/shard_map/ble,de->bld/dot_general | solution.py:124
  1162.8 49.0 %convolution_bitcast_fusion = f32[2048,2048]{1,0:T(8,128)} fusion(bf16[3,1536,2048]{2,1,0:T(8,128)(2,1)} %get-tuple-element.22, bf16[3,1536,2048]{2,1,0:T(8,128)(2,1)} %all-gather.9.cloned.1.call-done), kind=kOutput, calls=%fused_computation.51 | convolution fusion | flops 38654705664 | bytes 54525952 | tf_op jit(solution)/shard_map/blf,bld->fd/dot_general | solution.py:99
  1211.8 48.7 %convolution_bitcast_fusion.2 = f32[2048,2048]{1,0:T(8,128)} fusion(bf16[3,1536,2048]{2,1,0:T(8,128)(2,1)} %all-gather.7.cloned.1.call-done, bf16[3,1536,2048]{2,1,0:T(8,128)(2,1)} %get-tuple-element.21), kind=kOutput, calls=%fused_computation.53 | convolution fusion | flops 38654705664 | bytes 54525952 | tf_op jit(solution)/shard_map/bld,blf->df/dot_general | solution.py:104
  1260.6 56.9 %convolution_bitcast_fusion.1 = f32[2048,2048]{1,0:T(8,128)} fusion(bf16[3,1536,2048]{2,1,0:T(8,128)(2,1)} %all-gather.7.cloned.1.call-done, bf16[3,1536,2048]{2,1,0:T(8,128)(2,1)} %convolution_convert_fusion.1, f32[3,1536,2048]{2,1,0:T(8,128)} %get-tuple-element.37), kind=kOutput, calls=%fused_computation.52 | convolution fusion | flops 38758514688 | bytes 92274688 | tf_op jit(solution)/shard_map/bld,blf->df/dot_general | solution.py:105
  1317.5 11.0 convolution_bitcast_fusion.6
  1328.4 10.8 convolution_bitcast_fusion.5
  1339.3 11.1 convolution_bitcast_fusion.7
  1350.4 10.7 convolution_bitcast_fusion.4
  1361.1 3.7 fusion.42
  1364.8 25.4 %all-reduce.4 = (f32[2048]{0:T(1024)}, f32[2048]{0:T(1024)}) all-reduce(f32[2048]{0:T(1024)S(1)} %get-tuple-element.13, f32[2048]{0:T(1024)S(1)} %copy-done.41), channel_id=1, replica_groups=mesh['dp'=2,'tp'=8] {'tp'}, use_global_device_ids=true, to_apply=%region_12.13 | all-reduce | flops 4096 | bytes 32768 | tf_op jit(solution)/shard_map/psum | solution.py:127
  1390.2 5.3 add_convert_fusion.2
  1395.5 8.7 all-reduce.8.cloned.1.call-done
  1404.3 3.0 copy.66
  1407.3 3.0 copy.67
  (125 shorter events, 2.0 us)
Async XLA Ops:
  7.2 180.3 %copy-start = (bf16[256,2048]{1,0:T(8,128)(2,1)S(1)}, bf16[256,2048]{1,0:T(8,128)(2,1)}, u32[]{:S(2)}) copy-start(bf16[256,2048]{1,0:T(8,128)(2,1)} %param.21) | copy-start | bytes 3145732
  7.2 8.1 copy-start.50
  7.2 8.1 copy-start.49
  7.2 101.0 %all-gather.5.cloned.1.call-start = ((), (), s32[]{:S(2)}) async-start(), calls=%async_computation.4 | async-start | bytes 21233664 | tf_op jit(solution)/shard_map/all_gather | solution.py:48
  9.6 0.6 copy-start.37
  10.2 0.7 copy-start.33
  10.9 0.6 copy-start.27
  15.2 280.0 %reduce-scatter.5.cloned.1.call-start = ((), (), s32[]{:S(2)}) async-start(), calls=%async_computation.5 | async-start | bytes 21233664 | tf_op jit(solution)/shard_map/reduce_scatter | solution.py:52
  15.4 154.3 %copy-start.44 = (pred[3,1536]{1,0:T(4,128)(4,1)}, pred[3,1536]{1,0:T(4,128)(4,1)S(1)}, u32[]{:S(2)}) copy-start(pred[3,1536]{1,0:T(4,128)(4,1)S(1)} %get-tuple-element.40) | copy-start | bytes 13828
  15.4 154.3 %copy-start.46 = (pred[3,1536]{1,0:T(4,128)(4,1)}, pred[3,1536]{1,0:T(4,128)(4,1)S(1)}, u32[]{:S(2)}) copy-start(pred[3,1536]{1,0:T(4,128)(4,1)S(1)} %get-tuple-element.41) | copy-start | bytes 13828
  18.2 111.4 %copy-start.5 = (f32[1536,128]{0,1:T(8,128)}, f32[1536,128]{0,1:T(8,128)S(1)}, u32[]{:S(2)}) copy-start(f32[1536,128]{0,1:T(8,128)S(1)} %get-tuple-element.33) | copy-start | bytes 2359300
  18.2 111.4 %copy-start.7 = (f32[1536,128]{0,1:T(8,128)}, f32[1536,128]{0,1:T(8,128)S(1)}, u32[]{:S(2)}) copy-start(f32[1536,128]{0,1:T(8,128)S(1)} %get-tuple-element.34) | copy-start | bytes 2359300
  129.6 1.7 copy-start.9
  129.7 2.3 copy-start.24
  129.7 3.2 copy-start.25
  130.6 14.9 %copy-start.22 = (bf16[3,1536,128]{1,2,0:T(8,128)(2,1)}, bf16[3,1536,128]{1,2,0:T(8,128)(2,1)S(1)}, u32[]{:S(2)}) copy-start(bf16[3,1536,128]{1,2,0:T(8,128)(2,1)S(1)} %get-tuple-element.27) | copy-start | bytes 3538948
  130.6 14.9 %copy-start.23 = (bf16[3,1536,128]{1,2,0:T(8,128)(2,1)}, bf16[3,1536,128]{1,2,0:T(8,128)(2,1)S(1)}, u32[]{:S(2)}) copy-start(bf16[3,1536,128]{1,2,0:T(8,128)(2,1)S(1)} %get-tuple-element.28) | copy-start | bytes 3538948
  145.5 24.2 %copy-start.42 = (f32[3,1536]{1,0:T(4,128)}, f32[3,1536]{1,0:T(4,128)S(1)}, u32[]{:S(2)}) copy-start(f32[3,1536]{1,0:T(4,128)S(1)} %get-tuple-element.35) | copy-start | bytes 55300
  145.5 14.7 %copy-start.26 = (bf16[2048,256]{1,0:T(8,128)(2,1)S(1)}, bf16[2048,256]{1,0:T(8,128)(2,1)}, u32[]{:S(2)}) copy-start(bf16[2048,256]{1,0:T(8,128)(2,1)} %param.20) | copy-start | bytes 3145732
  160.2 9.5 copy-start.31
  169.7 16.4 %copy-start.51 = (bf16[3,1536,256]{2,1,0:T(8,128)(2,1)}, bf16[3,1536,256]{2,1,0:T(8,128)(2,1)S(1)}, u32[]{:S(2)}) copy-start(bf16[3,1536,256]{2,1,0:T(8,128)(2,1)S(1)} %convolution_convert_fusion.5) | copy-start | bytes 7077892
  186.1 1.4 copy-start.20
  196.7 0.9 copy-start.48
  196.8 98.5 %copy-start.1 = (bf16[3,192,2048]{2,1,0:T(8,128)(2,1)S(1)}, bf16[3,192,2048]{2,1,0:T(8,128)(2,1)}, u32[]{:S(2)}) copy-start(bf16[3,192,2048]{2,1,0:T(8,128)(2,1)} %param.13) | copy-start | bytes 7077892
  196.8 189.7 %all-gather.9.cloned.1.call-start = ((), (), s32[]{:S(2)}) async-start(), calls=%async_computation.8 | async-start | bytes 21233664 | tf_op jit(solution)/shard_map/all_gather | solution.py:48
  197.6 281.6 %all-gather.7.cloned.1.call-start = ((), (), s32[]{:S(2)}) async-start(), calls=%async_computation.6 | async-start | bytes 21233664 | tf_op jit(solution)/shard_map/all_gather | solution.py:48
  197.7 103.6 %copy-start.29 = (f32[2048]{0:T(1024)}, f32[2048]{0:T(1024)S(1)}, u32[]{:S(2)}) copy-start(f32[2048]{0:T(1024)S(1)} %convert_add_fusion.2) | copy-start | bytes 24580
  297.8 0.6 copy-start.39
  297.8 1.4 copy-start.3
  298.4 0.8 copy-start.35
  301.3 502.5 %reduce-scatter.9.cloned.1.call-start = ((), (), s32[]{:S(2)}) async-start(), calls=%async_computation.9 | async-start | bytes 21233664 | tf_op jit(solution)/shard_map/reduce_scatter | solution.py:52
  705.4 197.9 %reduce-scatter.7.cloned.1.call-start = ((), (), s32[]{:S(2)}) async-start(), calls=%async_computation.7 | async-start | bytes 21233664 | tf_op jit(solution)/shard_map/reduce_scatter | solution.py:52
  751.9 51.9 %copy-start.4 = (bf16[3,192,2048]{2,1,0:T(8,128)(2,1)S(1)}, bf16[3,192,2048]{2,1,0:T(8,128)(2,1)}, u32[]{:S(2)}) copy-start(bf16[3,192,2048]{2,1,0:T(8,128)(2,1)} %copy-done.3) | copy-start | bytes 7077892
  751.9 51.9 %copy-start.30 = (f32[2048]{0:T(1024)S(1)}, f32[2048]{0:T(1024)}, u32[]{:S(2)}) copy-start(f32[2048]{0:T(1024)} %copy-done.29) | copy-start | bytes 24580
  751.9 51.9 %copy-start.36 = (f32[3,192]{1,0:T(4,128)S(1)}, f32[3,192]{1,0:T(4,128)}, u32[]{:S(2)}) copy-start(f32[3,192]{1,0:T(4,128)} %copy-done.35) | copy-start | bytes 6916
  751.9 56.2 %copy-start.40 = (f32[3,192]{1,0:T(4,128)S(1)}, f32[3,192]{1,0:T(4,128)}, u32[]{:S(2)}) copy-start(f32[3,192]{1,0:T(4,128)} %copy-done.39) | copy-start | bytes 6916
  752.0 247.3 %all-gather.11.cloned.1.call-start = ((), (), s32[]{:S(2)}) async-start(), calls=%async_computation.10 | async-start | bytes 21233664 | tf_op jit(solution)/shard_map/all_gather | solution.py:48
  808.2 101.4 %copy-start.32 = (f32[3,1536]{1,0:T(4,128)S(1)}, f32[3,1536]{1,0:T(4,128)}, u32[]{:S(2)}) copy-start(f32[3,1536]{1,0:T(4,128)} %copy-done.31) | copy-start | bytes 55300
  909.5 451.6 %reduce-scatter.11.cloned.1.call-start = ((), (), s32[]{:S(2)}) async-start(), calls=%async_computation.11 | async-start | bytes 21233664 | tf_op jit(solution)/shard_map/reduce_scatter | solution.py:52
  909.6 100.5 %copy-start.10 = (pred[1536,1536]{0,1:T(8,128)(4,1)S(1)}, pred[1536,1536]{0,1:T(8,128)(4,1)}, u32[]{:S(2)}) copy-start(pred[1536,1536]{0,1:T(8,128)(4,1)} %iota_compare_fusion) | copy-start | bytes 7077892
  909.6 100.5 %copy-start.43 = (f32[3,1536]{1,0:T(4,128)S(1)}, f32[3,1536]{1,0:T(4,128)}, u32[]{:S(2)}) copy-start(f32[3,1536]{1,0:T(4,128)} %copy-done.42) | copy-start | bytes 55300
  909.6 100.5 %copy-start.45 = (pred[3,1536]{1,0:T(4,128)(4,1)S(1)}, pred[3,1536]{1,0:T(4,128)(4,1)}, u32[]{:S(2)}) copy-start(pred[3,1536]{1,0:T(4,128)(4,1)} %copy-done.44) | copy-start | bytes 13828
  909.6 100.5 %copy-start.47 = (pred[3,1536]{1,0:T(4,128)(4,1)S(1)}, pred[3,1536]{1,0:T(4,128)(4,1)}, u32[]{:S(2)}) copy-start(pred[3,1536]{1,0:T(4,128)(4,1)} %copy-done.46) | copy-start | bytes 13828
  1008.7 1.4 copy-start.52
  1071.6 21.0 %copy-start.6 = (f32[1536,128]{0,1:T(8,128)S(1)}, f32[1536,128]{0,1:T(8,128)}, u32[]{:S(2)}) copy-start(f32[1536,128]{0,1:T(8,128)} %copy-done.5) | copy-start | bytes 2359300
  1071.6 21.0 %copy-start.8 = (f32[1536,128]{0,1:T(8,128)S(1)}, f32[1536,128]{0,1:T(8,128)}, u32[]{:S(2)}) copy-start(f32[1536,128]{0,1:T(8,128)} %copy-done.7) | copy-start | bytes 2359300
  1092.6 2.3 copy-start.17
  1094.9 19.8 %copy-start.11 = (f32[3,1536,1,128]{1,3,0,2:T(8,128)}, f32[3,1536,1,128]{1,3,0,2:T(8,128)S(1)}, u32[]{:S(2)}) copy-start(f32[3,1536,1,128]{1,3,0,2:T(8,128)S(1)} %get-tuple-element.25) | copy-start | bytes 7077892
  1094.9 19.8 %copy-start.13 = (f32[3,1536,1,128]{1,3,0,2:T(8,128)}, f32[3,1536,1,128]{1,3,0,2:T(8,128)S(1)}, u32[]{:S(2)}) copy-start(f32[3,1536,1,128]{1,3,0,2:T(8,128)S(1)} %get-tuple-element.26) | copy-start | bytes 7077892
  1097.4 17.2 %copy-start.14 = (f32[3,1536,128]{1,2,0:T(8,128)}, f32[3,1536,128]{1,2,0:T(8,128)S(1)}, u32[]{:S(2)}) copy-start(f32[3,1536,128]{1,2,0:T(8,128)S(1)} %get-tuple-element.23) | copy-start | bytes 7077892
  1114.7 16.2 %copy-start.18 = (bf16[3,1536,256]{2,1,0:T(8,128)(2,1)S(1)}, bf16[3,1536,256]{2,1,0:T(8,128)(2,1)}, u32[]{:S(2)}) copy-start(bf16[3,1536,256]{2,1,0:T(8,128)(2,1)} %fusion.63) | copy-start | bytes 7077892
  1162.7 241.5 %all-reduce.8.cloned.1.call-start = ((), (), s32[]{:S(2)}) async-start(), calls=%async_computation.12 | async-start | bytes 8388608 | tf_op jit(solution)/shard_map/psum | solution.py:120
  1260.6 56.9 %copy-start.15 = (f32[3,1536,128]{1,2,0:T(8,128)S(1)}, f32[3,1536,128]{1,2,0:T(8,128)}, u32[]{:S(2)}) copy-start(f32[3,1536,128]{1,2,0:T(8,128)} %copy-done.14) | copy-start | bytes 7077892
  1260.6 56.9 %copy-start.16 = (f32[3,1536,128]{1,2,0:T(8,128)S(1)}, f32[3,1536,128]{1,2,0:T(8,128)}, u32[]{:S(2)}) copy-start(f32[3,1536,128]{1,2,0:T(8,128)} %get-tuple-element.24) | copy-start | bytes 7077892
  1317.4 11.0 copy-start.19
  1328.4 10.8 copy-start.12
  1339.3 11.1 copy-start.21
  1350.4 10.7 copy-start.2
  1350.4 10.7 copy-start.28
  1350.4 10.7 copy-start.34
  1350.4 14.5 %copy-start.41 = (f32[2048]{0:T(1024)S(1)}, f32[2048]{0:T(1024)}, u32[]{:S(2)}) copy-start(f32[2048]{0:T(1024)} %get-tuple-element.11) | copy-start | bytes 24580
  1350.4 39.8 %copy-start.38 = (f32[3,192]{1,0:T(4,128)S(1)}, f32[3,192]{1,0:T(4,128)}, u32[]{:S(2)}) copy-start(f32[3,192]{1,0:T(4,128)} %copy-done.37) | copy-start | bytes 6916
Sparse Core Ops, SparseCore 0:
  15.3 92.8 all-gather.4
  196.9 98.2 reduce-scatter.4
  296.8 89.6 all-gather.8
  388.5 90.6 all-gather.6
  705.5 98.2 reduce-scatter.8
  806.0 97.2 reduce-scatter.6
  909.6 89.6 all-gather.10
  1162.8 98.2 reduce-scatter.10
  1339.4 64.8 all-reduce.7
where the time goes:
time: 1420 us
  matrix products  741 us (52%)
  waiting for transfers between devices  563 us (40%)
  other arithmetic  56.8 us (4%)
  blocking collectives  25.4 us (2%)
  local copies, waits for them, and re-layouts  15.5 us (1%)
  between operations  14.7 us (1%)
    all_gather x4, waiting for transfers between devices, gather_seq(): return lax.all_gather(x_loc, 'tp', axis=1, tiled=True)  309 us
    reduce_scatter x4, waiting for transfers between devices, scatter_seq(): return lax.psum_scatter(x_part, 'tp', scatter_dimension=1, tiled=True)  244 us
    dot_general x1, matrix products, local_layer(): jnp.einsum('bld,df->blf', gated_all, w_gate, preferred_element_type=jnp.f...  77.4 us
    dot_general x1, matrix products, local_layer(): jnp.einsum('bld,blf->df', gated_all, d_upper, preferred_element_type=jnp....  56.9 us
    dot_general x3, matrix products, attend(): jnp.einsum('crie,cle->cirl', query, keys, preferred_element_type=jnp.floa...  56.8 us
    dot_general x3, matrix products, attend(): jnp.einsum('cirl,cle->crie', probs, values, preferred_element_type=jnp.fl...  54.6 us
    dot_general x1, matrix products, local_layer(): jnp.einsum('blf,df->bld', d_upper, w_up, preferred_element_type=jnp.float32)  54.3 us
    dot_general x1, matrix products, local_layer(): jnp.einsum('blf,bld->fd', act, grad_all, preferred_element_type=jnp.float32)  49 us
  transfers between devices with their start and end apart: 9, of which 8 were waited for; matrix products, arithmetic and copies ran while one was open for 22% of the time, Pallas kernels for 0%

commit v1 on v0

v1 whole, which is shorter than its diff:
```python
import math
import jax
import jax.numpy as jnp
from jax import lax
from jax.experimental import pallas as pl
from jax.experimental.pallas import tpu as pltpu
from jax.sharding import PartitionSpec as P

NORM_EPS = 1e-6
F32 = jnp.float32
BF16 = jnp.bfloat16
VMEM_LIMIT = 60 * 1024 * 1024
NN = (((1,), (0,)), ((), ()))
NT = (((1,), (1,)), ((), ()))
TN = (((0,), (0,)), ((), ()))


def dot(a, b, dims=NN):
    return lax.dot_general(a, b, dims, preferred_element_type=F32)


def rms_norm(x_in, gain):
    x_f = x_in.astype(F32)
    inv_rms = lax.rsqrt(jnp.mean(x_f * x_f, axis=-1, keepdims=True) + NORM_EPS)
    return (x_f * inv_rms * (1.0 + gain)).astype(BF16)


def rope_tables(positions, head_dim):
    half_dim = head_dim // 2
    exponent = jnp.arange(half_dim, dtype=F32) * (2.0 / head_dim)
    inv_freq = jnp.exp(exponent * (-math.log(10000.0)))
    angles = positions.astype(F32)[:, None] * inv_freq[None, :]
    return jnp.cos(angles), jnp.sin(angles)


def rotate(x_f, cos_t, sin_t):
    half_dim = x_f.shape[-1] // 2
    first = x_f[..., :half_dim]
    second = x_f[..., half_dim:]
    return jnp.concatenate([first * cos_t - second * sin_t, second * cos_t + first * sin_t], axis=-1)


def params(*semantics):
    return pltpu.CompilerParams(dimension_semantics=semantics, vmem_limit_bytes=VMEM_LIMIT)


def cost(flops, nbytes):
    return pl.CostEstimate(flops=int(flops), bytes_accessed=int(nbytes), transcendentals=0)


def rows_to_heads(x_in, weights, plane, group, tables=None):
    batch, rows, depth = x_in.shape
    heads, _, width, _ = weights.shape

    def kernel(x_ref, w_ref, *refs):
        o_ref = refs[-1]
        x_all = x_ref[...].reshape(batch * rows, depth)
        raw = dot(x_all, w_ref[...].reshape(group * width, depth), NT)
        for n in range(group):
            one = raw[:, n * width:(n + 1) * width].reshape(batch, rows, width)
            if tables is not None:
                one = rotate(one, refs[0][...], refs[1][...])
            o_ref[:, n] = one.astype(BF16)

    table_spec = pl.BlockSpec((rows, width // 2), lambda n: (0, 0))
    return pl.pallas_call(
        kernel,
        out_shape=jax.ShapeDtypeStruct((batch, heads, rows, width), BF16),
        grid=(heads // group,),
        in_specs=[
            pl.BlockSpec((batch, rows, depth), lambda n: (0, 0, 0)),
            pl.BlockSpec((group, 1, width, depth), lambda n: (n, plane, 0, 0)),
        ] + [table_spec] * (0 if tables is None else 2),
        out_specs=pl.BlockSpec((batch, group, rows, width), lambda n: (0, n, 0, 0)),
        compiler_params=params("arbitrary"),
        cost_estimate=cost(2 * batch * rows * depth * heads * width, 2 * heads * depth * width),
        name="rows_to_heads",
    )(x_in, weights, *(() if tables is None else tables))


def heads_to_rows(x_heads, weights, tile):
    batch, heads, rows, width = x_heads.shape
    depth = weights.shape[3]

    def kernel(x_ref, w_ref, o_ref):
        total = None
        for n in range(heads):
            term = dot(x_ref[:, n].reshape(batch * rows, width), w_ref[n, 0])
            total = term if total is None else total + term
        o_ref[...] = total.reshape(batch, rows, tile)

    return pl.pallas_call(
        kernel,
        out_shape=jax.ShapeDtypeStruct((batch, rows, depth), F32),
        grid=(depth // tile,),
        in_specs=[
            pl.BlockSpec((batch, heads, rows, width), lambda j: (0, 0, 0, 0)),
            pl.BlockSpec((heads, 1, width, tile), lambda j: (0, 1, 0, j)),
        ],
        out_specs=pl.BlockSpec((batch, rows, tile), lambda j: (0, 0, j)),
        compiler_params=params("arbitrary"),
        cost_estimate=cost(2 * batch * rows * depth * heads * width, 2 * heads * depth * width),
        name="heads_to_rows",
    )(x_heads, weights)


def input_grad(dq_heads, d_kv, weights, w_key, w_value, tile):
    batch, heads, rows, width = dq_heads.shape
    depth = weights.shape[3]

    def kernel(q_ref, kv_ref, w_ref, wk_ref, wv_ref, o_ref):
        kv_all = kv_ref[...].reshape(batch * rows, 2 * width)
        total = dot(kv_all[:, :width], wk_ref[...], NT) + dot(kv_all[:, width:], wv_ref[...], NT)
        for n in range(heads):
            total = total + dot(q_ref[:, n].reshape(batch * rows, width), w_ref[n, 0])
        o_ref[...] = total.reshape(batch, rows, tile).astype(BF16)

    return pl.pallas_call(
        kernel,
        out_shape=jax.ShapeDtypeStruct((batch, rows, depth), BF16),
        grid=(depth // tile,),
        in_specs=[
            pl.BlockSpec((batch, heads, rows, width), lambda j: (0, 0, 0, 0)),
            pl.BlockSpec((batch, rows, 2 * width), lambda j: (0, 0, 0)),
            pl.BlockSpec((heads, 1, width, tile), lambda j: (0, 0, 0, j)),
            pl.BlockSpec((tile, width), lambda j: (j, 0)),
            pl.BlockSpec((tile, width), lambda j: (j, 0)),
        ],
        out_specs=pl.BlockSpec((batch, rows, tile), lambda j: (0, 0, j)),
        compiler_params=params("arbitrary"),
        cost_estimate=cost(2 * batch * rows * depth * (heads + 2) * width, 2 * heads * depth * width),
        name="input_grad",
    )(dq_heads, d_kv, weights, w_key, w_value)


def out_weight_grad(mixed, d_rows):
    batch, heads, rows, width = mixed.shape
    depth = d_rows.shape[2]

    def kernel(a_ref, d_ref, o_ref):
        left = a_ref[:, 0].reshape(batch * rows, width).T
        o_ref[0] = dot(left, d_ref[...].reshape(batch * rows, depth))

    return pl.pallas_call(
        kernel,
        out_shape=jax.ShapeDtypeStruct((heads, width, depth), F32),
        grid=(heads,),
        in_specs=[
            pl.BlockSpec((batch, 1, rows, width), lambda n: (0, n, 0, 0)),
            pl.BlockSpec((batch, rows, depth), lambda n: (0, 0, 0)),
        ],
        out_specs=pl.BlockSpec((1, width, depth), lambda n: (n, 0, 0)),
        compiler_params=params("arbitrary"),
        cost_estimate=cost(2 * batch * rows * depth * heads * width, 4 * heads * depth * width),
        name="out_weight_grad",
    )(mixed, d_rows)


def query_weight_grad(normed, dq_heads):
    batch, heads, rows, width = dq_heads.shape
    depth = normed.shape[2]

    def kernel(u_ref, dq_ref, o_ref, ut_ref):
        @pl.when(pl.program_id(0) == 0)
        def _():
            ut_ref[...] = u_ref[...].reshape(batch * rows, depth).T

        o_ref[0] = dot(ut_ref[...], dq_ref[:, 0].reshape(batch * rows, width))

    return pl.pallas_call(
        kernel,
        out_shape=jax.ShapeDtypeStruct((heads, depth, width), F32),
        grid=(heads,),
        in_specs=[
            pl.BlockSpec((batch, rows, depth), lambda n: (0, 0, 0)),
            pl.BlockSpec((batch, 1, rows, width), lambda n: (0, n, 0, 0)),
        ],
        out_specs=pl.BlockSpec((1, depth, width), lambda n: (n, 0, 0)),
        scratch_shapes=[pltpu.VMEM((depth, batch * rows), BF16)],
        compiler_params=params("arbitrary"),
        cost_estimate=cost(2 * batch * rows * depth * heads * width, 4 * heads * depth * width),
        name="query_weight_grad",
    )(normed, dq_heads)


def fill_bias(lens_ref, bias_ref, rows, c):
    first, prefix, valid = lens_ref[0], lens_ref[1 + 2 * c], lens_ref[2 + 2 * c]
    key_pos = lax.broadcasted_iota(jnp.int32, bias_ref.shape, 0)
    column = lax.broadcasted_iota(jnp.int32, bias_ref.shape, 1)
    q_pos = first + lax.rem(column, rows)
    visible = (key_pos < valid) & ((key_pos < prefix) | (key_pos <= q_pos))
    bias_ref[...] = jnp.where(visible, 0.0, -1e30).astype(F32)


def attention_fwd(q_heads, keys_values, lens, group, block):
    batch, heads, rows, width = q_heads.shape
    length = keys_values.shape[1]
    cols = group * rows
    scale = width ** -0.5

    def kernel(lens_ref, q_ref, k_ref, v_ref, o_ref, lse_ref, bias_ref, vt_ref, score_ref):
        c, g = pl.program_id(0), pl.program_id(1)

        @pl.when(g == 0)
        def _():
            fill_bias(lens_ref, bias_ref, rows, c)
            vt_ref[...] = v_ref[0].T

        q_s = q_ref[0].reshape(cols, width) * jnp.asarray(scale, BF16)
        top = jnp.full((1, cols), -jnp.inf, F32)
        for at in range(0, length, block):
            scores = dot(k_ref[0, at:at + block], q_s, NT) + bias_ref[at:at + block]
            score_ref[at:at + block] = scores
            top = jnp.maximum(top, jnp.max(scores, axis=0, keepdims=True))
        total = jnp.zeros((1, cols), F32)
        for at in range(0, length, block):
            probs = jnp.exp(score_ref[at:at + block] - top)
            score_ref[at:at + block] = probs
            total = total + jnp.sum(probs, axis=0, keepdims=True)
        lse_ref[0] = top + jnp.log(total)
        inverse = 1.0 / total
        out = None
        for at in range(0, length, block):
            term = dot(vt_ref[:, at:at + block], (score_ref[at:at + block] * inverse).astype(BF16))
            out = term if out is None else out + term
        o_ref[0] = out.T.astype(BF16).reshape(group, rows, width)

    return pl.pallas_call(
        kernel,
        out_shape=(
            jax.ShapeDtypeStruct((batch, heads, rows, width), BF16),
            jax.ShapeDtypeStruct((batch, 1, heads * rows), F32),
        ),
        grid_spec=pltpu.PrefetchScalarGridSpec(
            num_scalar_prefetch=1,
            grid=(batch, heads // group),
            in_specs=[
                pl.BlockSpec((1, group, rows, width), lambda c, g, s: (c, g, 0, 0)),
                pl.BlockSpec((1, length, width), lambda c, g, s: (c, 0, 0)),
                pl.BlockSpec((1, length, width), lambda c, g, s: (c, 0, 1)),
            ],
            out_specs=(
                pl.BlockSpec((1, group, rows, width), lambda c, g, s: (c, g, 0, 0)),
                pl.BlockSpec((1, 1, cols), lambda c, g, s: (c, 0, g)),
            ),
            scratch_shapes=[pltpu.VMEM((length, cols), F32), pltpu.VMEM((width, length), BF16), pltpu.VMEM((length, cols), F32)],
        ),
        compiler_params=params("arbitrary", "arbitrary"),
        cost_estimate=cost(4 * batch * heads * rows * length * width, 16 * batch * heads * rows * width),
        name="attention_fwd",
    )(lens, q_heads, keys_values, keys_values)


def attention_bwd(q_heads, keys_values, mixed, d_mixed, lse, cos_t, sin_t, lens, group, block, start):
    _, heads, rows, width = q_heads.shape
    batch = d_mixed.shape[0]
    length = keys_values.shape[1]
    cols = group * rows
    groups = heads // group
    scale = width ** -0.5

    def kernel(lens_ref, q_ref, k_ref, v_ref, mixed_ref, dm_ref, lse_ref, cos_ref, sin_ref, dq_ref, dkv_ref, bias_ref, kt_ref, acc_ref):
        c, g = pl.program_id(0), pl.program_id(1)

        @pl.when(g == 0)
        def _():
            fill_bias(lens_ref, bias_ref, rows, c + start)
            kt_ref[...] = k_ref[0].T
            acc_ref[...] = jnp.zeros_like(acc_ref)

        q_s = q_ref[0].reshape(cols, width) * jnp.asarray(scale, BF16)
        d_m = dm_ref[0].reshape(cols, width)
        inner = d_m.astype(F32) * mixed_ref[0].reshape(cols, width).astype(F32)
        inner = jnp.sum(inner.T, axis=0, keepdims=True)
        d_q = None
        for at in range(0, length, block):
            here = slice(at, at + block)
            probs = jnp.exp(dot(k_ref[0, here], q_s, NT) + bias_ref[here] - lse_ref[0])
            d_scores = (probs * (dot(v_ref[0, here], d_m, NT) - inner)).astype(BF16)
            acc_ref[here, :width] += dot(d_scores, q_s)
            acc_ref[here, width:] += dot(probs.astype(BF16), d_m)
            term = dot(kt_ref[:, here], d_scores)
            d_q = term if d_q is None else d_q + term
        d_q = (d_q * scale).T.reshape(group, rows, width)
        dq_ref[0] = rotate(d_q, cos_ref[...], -sin_ref[...]).astype(BF16)

        @pl.when(g == groups - 1)
        def _():
            dkv_ref[0] = acc_ref[...].astype(BF16)

    return pl.pallas_call(
        kernel,
        out_shape=(
            jax.ShapeDtypeStruct((batch, heads, rows, width), BF16),
            jax.ShapeDtypeStruct((batch, length, 2 * width), BF16),
        ),
        grid_spec=pltpu.PrefetchScalarGridSpec(
            num_scalar_prefetch=1,
            grid=(batch, groups),
            in_specs=[
                pl.BlockSpec((1, group, rows, width), lambda c, g, s: (c + start, g, 0, 0)),
                pl.BlockSpec((1, length, width), lambda c, g, s: (c + start, 0, 0)),
                pl.BlockSpec((1, length, width), lambda c, g, s: (c + start, 0, 1)),
                pl.BlockSpec((1, group, rows, width), lambda c, g, s: (c + start, g, 0, 0)),
                pl.BlockSpec((1, group, rows, width), lambda c, g, s: (c, g, 0, 0)),
                pl.BlockSpec((1, 1, cols), lambda c, g, s: (c + start, 0, g)),
                pl.BlockSpec((rows, width // 2), lambda c, g, s: (0, 0)),
                pl.BlockSpec((rows, width // 2), lambda c, g, s: (0, 0)),
            ],
            out_specs=(
                pl.BlockSpec((1, group, rows, width), lambda c, g, s: (c, g, 0, 0)),
                pl.BlockSpec((1, length, 2 * width), lambda c, g, s: (c, 0, 0)),
            ),
            scratch_shapes=[
                pltpu.VMEM((length, cols), F32),
                pltpu.VMEM((width, length), BF16),
                pltpu.VMEM((length, 2 * width), F32),
            ],
        ),
        compiler_params=params("arbitrary", "arbitrary"),
        cost_estimate=cost(10 * batch * heads * rows * length * width, 16 * batch * heads * rows * width),
        name="attention_bwd",
    )(lens, q_heads, keys_values, keys_values, mixed, d_mixed, lse, cos_t, sin_t)


def gelu_and_slope(gate):
    root = math.sqrt(2.0 / math.pi)
    square = gate * gate
    tanh = jnp.tanh(root * gate * (1.0 + 0.044715 * square))
    half = 0.5 * (1.0 + tanh)
    slope = half + 0.5 * gate * (1.0 - tanh * tanh) * (root * (1.0 + 3 * 0.044715 * square))
    return gate * half, slope


def mlp_core(z_seq, g_seq, w_gate, w_up, w_down, tm, tn):
    _, rows, depth = z_seq[0].shape
    width = w_gate.shape[1]

    def kernel(z_ref, g_ref, wg_ref, wu_ref, wd_ref, act_ref, dg_ref, du_ref):
        gate = dot(z_ref[0], wg_ref[...])
        upper = dot(z_ref[0], wu_ref[...])
        d_act = dot(g_ref[0], wd_ref[...], NT).astype(BF16).astype(F32)
        gelu, slope = gelu_and_slope(gate)
        act_ref[...] = (gelu * upper).astype(BF16)
        dg_ref[...] = (d_act * upper * slope).astype(BF16)
        du_ref[...] = (d_act * gelu).astype(BF16)

    def row_spec(k):
        return pl.BlockSpec((1, tm, depth), lambda i, j: (k, i, 0))

    col_spec = pl.BlockSpec((depth, tn), lambda i, j: (0, j))
    out_spec = pl.BlockSpec((tm, tn), lambda i, j: (i, j))
    out = jax.ShapeDtypeStruct((rows, width), BF16)
    return pl.pallas_call(
        kernel,
        out_shape=(out, out, out),
        grid=(rows // tm, width // tn),
        in_specs=[row_spec(z_seq[1]), row_spec(g_seq[1]), col_spec, col_spec, pl.BlockSpec((tn, depth), lambda i, j: (j, 0))],
        out_specs=(out_spec, out_spec, out_spec),
        compiler_params=params("arbitrary", "arbitrary"),
        cost_estimate=cost(6 * rows * depth * width, 6 * depth * width + 10 * rows * depth),
        name="mlp_core",
    )(z_seq[0], g_seq[0], w_gate, w_up, w_down)


def product_sum(lefts, rights, dims, out_dtype, tm, tn):
    rows, depth = lefts[0].shape
    width = rights[0].shape[0] if dims == NT else rights[0].shape[1]
    count = len(lefts)

    def kernel(*refs):
        total = dot(refs[0][...], refs[count][...], dims)
        for i in range(1, count):
            total = total + dot(refs[i][...], refs[count + i][...], dims)
        refs[-1][...] = total.astype(out_dtype)

    left_spec = pl.BlockSpec((tm, depth), lambda i, j: (i, 0))
    if dims == NT:
        right_spec = pl.BlockSpec((tn, depth), lambda i, j: (j, 0))
    else:
        right_spec = pl.BlockSpec((depth, tn), lambda i, j: (0, j))
    return pl.pallas_call(
        kernel,
        out_shape=jax.ShapeDtypeStruct((rows, width), out_dtype),
        grid=(rows // tm, width // tn),
        in_specs=[left_spec] * count + [right_spec] * count,
        out_specs=pl.BlockSpec((tm, tn), lambda i, j: (i, j)),
        compiler_params=params("arbitrary", "arbitrary"),
        cost_estimate=cost(2 * count * rows * depth * width, 2 * count * depth * (rows + width)),
    )(*lefts, *rights)


def split_product(lefts, right, core, chips, tm, tn):
    rows, depth = lefts[0].shape
    width = right.shape[1]
    count, steps = len(lefts), rows // tm
    shard = rows // (2 * chips)
    here = tm // (2 * shard)

    def kernel(core_ref, *refs):
        c = pl.program_id(0)
        for k in range(count):
            @pl.when(c == k)
            def _(k=k):
                product = dot(refs[k][...], refs[count][...]).astype(BF16).reshape(here, 2, shard, tn)
                first = core_ref[0] == 0
                refs[-2][:, 0] = jnp.where(first, product[:, 0], product[:, 1])
                refs[-1][:, 0] = jnp.where(first, product[:, 1], product[:, 0])

    def left_spec(k):
        return pl.BlockSpec((tm, depth), lambda c, i, j, s: (jnp.where(c == k, i, jnp.where(c < k, 0, steps - 1)), 0))

    out = jax.ShapeDtypeStruct((chips, count, shard, width), BF16)
    out_spec = pl.BlockSpec((here, 1, shard, tn), lambda c, i, j, s: (i, c, 0, j))
    return pl.pallas_call(
        kernel,
        out_shape=(out, out),
        grid_spec=pltpu.PrefetchScalarGridSpec(
            num_scalar_prefetch=1,
            grid=(count, steps, width // tn),
            in_specs=[left_spec(k) for k in range(count)] + [pl.BlockSpec((depth, tn), lambda c, i, j, s: (0, j))],
            out_specs=(out_spec, out_spec),
        ),
        compiler_params=params("arbitrary", "arbitrary", "arbitrary"),
        cost_estimate=cost(2 * count * rows * depth * width, 2 * count * rows * (depth + width)),
        name="mlp_out",
    )(core[None], *lefts, right)


def weight_grad(lefts, rights, tm, tn):
    _, rows, depth = lefts[0][0].shape
    width = rights[0][0].shape[2]
    count = len(lefts)

    def kernel(*refs):
        total = None
        for c in range(count):
            term = dot(refs[c][0], refs[count + c][0], TN)
            total = term if total is None else total + term
        refs[-1][...] = total

    def left_spec(k):
        return pl.BlockSpec((1, rows, tm), lambda i, j: (k, 0, i))

    def right_spec(k):
        return pl.BlockSpec((1, rows, tn), lambda i, j: (k, 0, j))

    return pl.pallas_call(
        kernel,
        out_shape=jax.ShapeDtypeStruct((depth, width), F32),
        grid=(depth // tm, width // tn),
        in_specs=[left_spec(k) for _, k in lefts] + [right_spec(k) for _, k in rights],
        out_specs=pl.BlockSpec((tm, tn), lambda i, j: (i, j)),
        compiler_params=params("arbitrary", "arbitrary"),
        cost_estimate=cost(2 * count * rows * depth * width, 2 * count * rows * (depth + width)),
        name="weight_grad",
    )(*[a for a, _ in lefts], *[a for a, _ in rights])


def chip_shift(x_in, step, size):
    return lax.ppermute(x_in, "tp", [(t, (t + 2 * step) % size) for t in range(size)])


def swap_cores(x_in, size):
    return lax.ppermute(x_in, "tp", [(t, t ^ 1) for t in range(size)])


def scatter_by_sends(keep, arrived, chip, size, marks):
    chips, count, shard, depth = keep.shape
    half = shard // 2
    arrived = after(arrived, marks[0])

    def pair_sum(step):
        at = ((chip + step) % chips, 0, 0, 0)
        cut = (1, count, shard, depth)
        return lax.dynamic_slice(keep, at, cut)[0].astype(F32) + lax.dynamic_slice(arrived, at, cut)[0].astype(F32)

    far = pair_sum(2).astype(BF16)
    far_low = after(chip_shift(far[:, :half], 1, size), marks[1])
    far_high = after(chip_shift(far[:, half:], -1, size), marks[1])
    forward, backward = pair_sum(1), pair_sum(-1)
    forward = jnp.concatenate([forward[:, :half] + far_low.astype(F32), forward[:, half:]], axis=1).astype(BF16)
    backward = jnp.concatenate([backward[:, :half], backward[:, half:] + far_high.astype(F32)], axis=1).astype(BF16)
    forward = after(chip_shift(forward, 1, size), marks[2])
    backward = after(chip_shift(backward, -1, size), marks[2])
    return pair_sum(0) + forward.astype(F32) + backward.astype(F32)


def gather(x_loc, axis):
    return lax.all_gather(x_loc, "tp", axis=axis, tiled=True)


def after(value, earlier):
    return lax.optimization_barrier((value, earlier))[0]


def scatter(x_part, axis):
    return lax.psum_scatter(x_part, "tp", scatter_dimension=axis, tiled=True)


def solution(mesh):
    tp_size = mesh.shape["tp"]
    act_spec = P("dp", "tp", None)
    in_specs = (act_spec, act_spec, P("dp"), P("dp"), P(None), P(None, "tp"), P(None, None), P(None, None), P("tp", None), P(None), P(None, "tp"), P(None, "tp"), P("tp", None))
    out_specs = (act_spec, act_spec, P("dp"), P("dp", "tp"), P("dp", None), P("dp", None), P(("dp", "tp"), None), P("dp"), P("dp", "tp"), P("dp", "tp"), P(("dp", "tp"), None))

    def local_layer(hidden, grad_out, prefix_len, valid_len, attn_norm, w_query, w_key, w_value, w_out, mlp_norm, w_gate, w_up, w_down):
        batch, shard_len, model_dim = hidden.shape
        head_dim = w_key.shape[1]
        heads = tp_size * w_query.shape[1] // head_dim
        first = lax.axis_index("tp") * shard_len
        cos_t, sin_t = rope_tables(first + jnp.arange(shard_len), head_dim)
        lens = jnp.concatenate([first[None].astype(jnp.int32), jnp.stack([prefix_len, valid_len], axis=1).reshape(-1).astype(jnp.int32)])

        weights = gather(jnp.stack([w_query.T, w_out])[None], 0)
        normed, norm1_pull = jax.vjp(rms_norm, hidden, attn_norm.astype(F32))
        k_raw = jnp.einsum("bsd,de->bse", normed, w_key, preferred_element_type=F32)
        keys = rotate(k_raw, cos_t, sin_t).astype(BF16)
        values = jnp.einsum("bsd,de->bse", normed, w_value, preferred_element_type=F32).astype(BF16)
        keys_values = gather(jnp.concatenate([keys, values], axis=-1), 1)
        query = rows_to_heads(normed, weights, 0, 2, (cos_t, sin_t))
        mixed, lse = attention_fwd(query, keys_values, lens, 4, 512)
        attn_out = heads_to_rows(mixed, weights, 1024)
        resid = (hidden.astype(F32) + attn_out).astype(BF16)
        gated_in = rms_norm(resid, mlp_norm.astype(F32))

        me = lax.axis_index("tp")
        chip, core = me // 2, me % 2
        z_all, g_all, acts, d_gates, d_ups, d_gated = [], [], [], [], [], []
        for c in range(batch):
            g_c = (gather(grad_out[c:c + 1], 1), 0)
            z_c = (gather(gated_in[c:c + 1], 1), 0)
            if c:
                z_c = (after(z_c[0], d_z_part), 0)
            act, d_gate, d_up = mlp_core(z_c, g_c, w_gate, w_up, w_down, 768, 512)
            d_z_part = product_sum([d_gate, d_up], [w_gate, w_up], NT, BF16, 768, 1024)
            d_gated.append(scatter(d_z_part, 0))
            for items, item in zip((z_all, g_all, acts, d_gates, d_ups), (z_c, g_c, act, d_gate, d_up)):
                items.append(item)

        def planes(arrays):
            return [(a[None], 0) for a in arrays]

        d_resids, norm_parts, dq_parts, d_kv_sums = [], [], [], []
        previous = d_z_part
        for start, stop in ((0, batch - 1), (batch - 1, batch)):
            _, norm2_pull = jax.vjp(rms_norm, resid[start:stop], mlp_norm.astype(F32))
            d_resid_norm, norm_part = norm2_pull(after(jnp.stack(d_gated[start:stop]), previous))
            d_resid = (grad_out[start:stop].astype(F32) + d_resid_norm.astype(F32)).astype(BF16)
            d_mixed = rows_to_heads(d_resid, weights, 1, 2)
            dq_part, d_kv_part = attention_bwd(query, keys_values, mixed, d_mixed, lse, cos_t, sin_t, lens, 4, 512, start)
            d_kv_sums.append(scatter(d_kv_part, 1))
            previous = d_kv_part
            d_resids.append(d_resid)
            norm_parts.append(norm_part)
            dq_parts.append(dq_part)
        d_resid = jnp.concatenate(d_resids, axis=0)
        g_mlp_norm_part = norm_parts[0] + norm_parts[1]
        dq_raw = jnp.concatenate(dq_parts, axis=0)
        d_kv = jnp.concatenate(d_kv_sums, axis=0)

        g_query_part = query_weight_grad(after(normed, d_kv_part), dq_raw)
        g_query = scatter(g_query_part, 0)[0]
        keep, send = split_product(after(acts, g_query_part), w_down, core, tp_size // 2, 768, 1024)
        arrived = swap_cores(send, tp_size)
        d_kv = after(d_kv, keep)
        d_k_raw = rotate(d_kv[..., :head_dim].astype(F32), cos_t, -sin_t).astype(BF16)
        d_kv_raw = jnp.concatenate([d_k_raw, d_kv[..., head_dim:]], axis=-1)
        d_normed = input_grad(dq_raw, d_kv_raw, weights, w_key, w_value, 1024)
        d_hidden_norm, g_attn_norm_part = norm1_pull(d_normed)
        grad_hidden = (d_resid.astype(F32) + d_hidden_norm.astype(F32)).astype(BF16)

        g_kv_part = jnp.einsum("bsd,bse->de", normed, d_kv_raw, preferred_element_type=F32)
        norms = jnp.concatenate([g_attn_norm_part, g_mlp_norm_part]).reshape(-1, 2 * head_dim)
        count = norms.shape[0]
        fill = jnp.zeros((-(model_dim + count) % (8 * heads), 2 * head_dim), F32)
        small_part = jnp.concatenate([g_kv_part, norms, fill], axis=0)
        small = scatter(small_part, 0)
        g_out_part = out_weight_grad(after(mixed, small_part), d_resid)
        g_out = scatter(g_out_part, 0)

        g_down = weight_grad(planes(after(acts, g_out_part)), g_all, 1024, 512)
        g_gate = weight_grad(z_all, planes(after(d_gates, g_down)), 1024, 512)
        g_up = weight_grad(z_all, planes(after(d_ups, g_gate)), 1024, 512)
        mlp_sum = scatter_by_sends(keep, arrived, chip, tp_size, (small_part, g_down, g_up)).astype(BF16)
        hidden_out = (resid.astype(F32) + mlp_sum.astype(F32)).astype(BF16)
        small = gather(after(small, g_gate), 0)
        g_key, g_value = small[:model_dim, :head_dim], small[:model_dim, head_dim:]
        g_norms = small[model_dim:model_dim + count].reshape(2, model_dim)

        return (hidden_out, grad_hidden, g_norms[0], g_query, g_key, g_value, g_out.reshape(-1, model_dim), g_norms[1], g_gate, g_up, g_down)

    return jax.shard_map(local_layer, mesh=mesh, in_specs=in_specs, out_specs=out_specs, check_vma=False)
```

time: 1420 us -> 1020 us (0.72)
  matrix products: 741 us -> 5.41 us
  Pallas kernels: 0 us -> 569 us
  waiting for transfers between devices: 563 us -> 322 us
  blocking collectives: 25.4 us -> 0 us
  local copies, waits for them, and re-layouts: 15.5 us -> 38.7 us
    dot_general x27 -> x3, matrix products: 741 us -> 5.41 us  [the longest x1 3.86 us: local_layer(): jnp.einsum('bsd,bse->de', normed, d_kv_raw, preferred_element_type=F32)]
    pallas_call x0 -> x20, Pallas kernels: none -> 569 us  [the longest x3 145 us: mlp_core(): pl.pallas_call(kernel, out_shape=(out, out, out), grid=(rows // tm, width...]
    all_gather x4 -> x9, waiting for transfers between devices: 309 us -> 130 us  [gather(): return lax.all_gather(x_loc, 'tp', axis=axis, tiled=True)]
    reduce_scatter x4 -> x8, waiting for transfers between devices: 244 us -> 107 us  [scatter(): return lax.psum_scatter(x_part, 'tp', scatter_dimension=axis, tiled=True)]
    ppermute x0 -> x5, waiting for transfers between devices: none -> 79.6 us  [the longest x4 62.9 us: chip_shift(): lax.ppermute(x_in, 'tp', [(t, (t + 2 * step) % size) for t in range(size)])]
    psum x1 -> x0, blocking collectives: 25.4 us -> none  [local_layer(): g_attn_norm = lax.psum(g_attn_norm_part, 'tp')]
    reduce_sum x3, other arithmetic: 22.8 us -> 7.01 us  [rms_norm(): return (x_f * inv_rms * (1.0 + gain)).astype(BF16)]
  transfers between devices with their start and end apart: 9 -> 22, of which waited for: 8 -> 11; matrix products, arithmetic and copies ran while one was open for 22% -> 6% of each run, Pallas kernels for 0% -> 53%
where the time goes in v1:
time: 1020 us
  Pallas kernels  569 us (56%)
  waiting for transfers between devices  322 us (32%)
  other arithmetic  61.1 us (6%)
  local copies, waits for them, and re-layouts  38.7 us (4%)
  between operations  14.7 us (1%)
    pallas_call x3, Pallas kernels, mlp_core(): pl.pallas_call(kernel, out_shape=(out, out, out), grid=(rows // tm, width...  145 us
    pallas_call x3, Pallas kernels, weight_grad(): pl.pallas_call(kernel, out_shape=jax.ShapeDtypeStruct((depth, width), F32...  144 us
    all_gather x9, waiting for transfers between devices, gather(): return lax.all_gather(x_loc, 'tp', axis=axis, tiled=True)  130 us
    reduce_scatter x8, waiting for transfers between devices, scatter(): return lax.psum_scatter(x_part, 'tp', scatter_dimension=axis, tiled=True)  107 us
    pallas_call x3, Pallas kernels, product_sum(): pl.pallas_call(kernel, out_shape=jax.ShapeDtypeStruct((rows, width), out_...  101 us
    ppermute x4, waiting for transfers between devices, chip_shift(): lax.ppermute(x_in, 'tp', [(t, (t + 2 * step) % size) for t in range(size)])  62.9 us
    pallas_call x1, Pallas kernels, split_product(): pl.pallas_call(kernel, out_shape=(out, out), grid_spec=pltpu.PrefetchScal...  49 us
    pallas_call x2, Pallas kernels, attention_bwd(): pl.pallas_call(kernel, out_shape=(jax.ShapeDtypeStruct((batch, heads, row...  35.8 us
  transfers between devices with their start and end apart: 22, of which 11 were waited for; matrix products, arithmetic and copies ran while one was open for 6% of the time, Pallas kernels for 53%

profile of v1, /device:TPU:112, one launch (start us, length us, event | category | flops | bytes accessed | tf_op | source)
XLA Modules:
  0.0 1018.8 jit_solution(15652444809055725344)
XLA Ops:
  7.3 1.5 copy.29
  8.8 2.9 pad_maximum_fusion.3
  13.0 1.1 fusion.30
  18.1 0.9 pad_maximum_fusion.5
  19.1 3.4 fusion.37
  23.6 71.9 %all-gather.27.cloned.1.call-done = bf16[16,256,2048]{2,1,0:T(8,128)(2,1)} async-done(((bf16[2,256,2048]{2,1,0:T(8,128)(2,1)}), bf16[16,256,2048]{2,1,0:T(8,128)(2,1)}) %all-gather.27.cloned.1.call-update) | async-done | bytes 16777232 | tf_op jit(solution)/shard_map/all_gather | solution.py:490
  95.6 9.4 rows_to_heads.3.q_ref
  104.9 23.6 %all-gather.11.cloned.1.call-done.k_ref.v_ref = bf16[3,1536,512]{2,1,0:T(8,128)(2,1)} async-done(((bf16[3,192,512]{2,1,0:T(8,128)(2,1)}), bf16[3,1536,512]{2,1,0:T(8,128)(2,1)}) %all-gather.11.cloned.1.call-update) | async-done | bytes 4718608 | tf_op jit(solution)/shard_map/all_gather | solution.py:490
  128.5 24.0 %attention_fwd.1 = (bf16[3,8,192,256]{3,2,1,0:T(8,128)(2,1)}, f32[3,1,1536]{2,1,0:T(1,128)}) custom-call(s32[7]{0:T(128)} %pad_add_fusion.1.lens_ref, bf16[3,8,192,256]{3,2,1,0:T(8,128)(2,1)} %rows_to_heads.3.q_ref, bf16[3,1536,512]{2,1,0:T(8,128)(2,1)} %all-gather.11.cloned.1.call-done.k_ref.v_ref, ...), custom_call_target="tpu_custom_call" | custom-call | flops 7247757312 | bytes 18874368 | tf_op jit(solution)/shard_map/attention_fwd/pallas_call | solution.py:228
  152.5 9.7 heads_to_rows.1
  162.2 3.2 fusion.4
  166.8 1.5 fusion.38
  171.5 34.7 %all-gather.13.cloned.1.call-done.z_ref.refs_0_ = bf16[1,1536,2048]{2,1,0:T(8,128)(2,1)} async-done(((bf16[1,192,2048]{2,1,0:T(8,128)(2,1)}), bf16[1,1536,2048]{2,1,0:T(8,128)(2,1)}) %all-gather.13.cloned.1.call-update) | async-done | bytes 6291472 | tf_op jit(solution)/shard_map/all_gather | solution.py:490
  206.3 47.8 %mlp_core.3 = (bf16[1536,2048]{1,0:T(8,128)(2,1)}, bf16[1536,2048]{1,0:T(8,128)(2,1)}, bf16[1536,2048]{1,0:T(8,128)(2,1)}) custom-call(bf16[1,1536,2048]{2,1,0:T(8,128)(2,1)} %all-gather.13.cloned.1.call-done.z_ref.refs_0_, bf16[1,1536,2048]{2,1,0:T(8,128)(2,1)} %all-gather.15.cloned.1.call-done.g_ref.refs_3_, bf16[2048,2048]{1,0:T(8,128)(2,1)} %refs_2_.5, ...), custom_call_target="tpu_custom_call" | custom-call | flops 38654705664 | bytes 56623104 | tf_op jit(solution)/shard_map/mlp_core/pallas_call | solution.py:354
  254.1 33.4 %shard_map.212 = bf16[1536,2048]{1,0:T(8,128)(2,1)} custom-call(bf16[1536,2048]{1,0:T(8,128)(2,1)} %get-tuple-element.85.refs_0_, bf16[1536,2048]{1,0:T(8,128)(2,1)} %get-tuple-element.88.refs_1_, bf16[2048,2048]{1,0:T(8,128)(2,1)} %refs_2_.5, bf16[2048,2048]{1,0:T(8,128)(2,1)} %refs_3_.6), custom_call_target="tpu_custom_call" | custom-call | flops 25769803776 | bytes 29360128 | tf_op jit(solution)/shard_map/pallas_call | solution.py:382
  287.9 49.1 %mlp_core.4 = (bf16[1536,2048]{1,0:T(8,128)(2,1)}, bf16[1536,2048]{1,0:T(8,128)(2,1)}, bf16[1536,2048]{1,0:T(8,128)(2,1)}) custom-call(bf16[1,1536,2048]{2,1,0:T(8,128)(2,1)} %all-gather.17.cloned.1.call-done.z_ref.refs_1_, bf16[1,1536,2048]{2,1,0:T(8,128)(2,1)} %all-gather.19.cloned.1.call-done.g_ref.refs_4_, bf16[2048,2048]{1,0:T(8,128)(2,1)} %refs_2_.5, ...), custom_call_target="tpu_custom_call" | custom-call | flops 38654705664 | bytes 56623104 | tf_op jit(solution)/shard_map/mlp_core/pallas_call | solution.py:354
  337.0 33.5 %shard_map.213 = bf16[1536,2048]{1,0:T(8,128)(2,1)} custom-call(bf16[1536,2048]{1,0:T(8,128)(2,1)} %get-tuple-element.86.refs_0_, bf16[1536,2048]{1,0:T(8,128)(2,1)} %get-tuple-element.89.refs_1_, bf16[2048,2048]{1,0:T(8,128)(2,1)} %refs_2_.5, bf16[2048,2048]{1,0:T(8,128)(2,1)} %refs_3_.6), custom_call_target="tpu_custom_call" | custom-call | flops 25769803776 | bytes 29360128 | tf_op jit(solution)/shard_map/pallas_call | solution.py:382
  371.2 48.1 %mlp_core.5 = (bf16[1536,2048]{1,0:T(8,128)(2,1)}, bf16[1536,2048]{1,0:T(8,128)(2,1)}, bf16[1536,2048]{1,0:T(8,128)(2,1)}) custom-call(bf16[1,1536,2048]{2,1,0:T(8,128)(2,1)} %all-gather.21.cloned.1.call-done.z_ref.refs_2_, bf16[1,1536,2048]{2,1,0:T(8,128)(2,1)} %all-gather.23.cloned.1.call-done.g_ref.refs_5_, bf16[2048,2048]{1,0:T(8,128)(2,1)} %refs_2_.5, ...), custom_call_target="tpu_custom_call" | custom-call | flops 38654705664 | bytes 56623104 | tf_op jit(solution)/shard_map/mlp_core/pallas_call | solution.py:354
  419.3 33.6 %shard_map.214 = bf16[1536,2048]{1,0:T(8,128)(2,1)} custom-call(bf16[1536,2048]{1,0:T(8,128)(2,1)} %get-tuple-element.87.refs_0_, bf16[1536,2048]{1,0:T(8,128)(2,1)} %get-tuple-element.90.refs_1_, bf16[2048,2048]{1,0:T(8,128)(2,1)} %refs_2_.5, bf16[2048,2048]{1,0:T(8,128)(2,1)} %refs_3_.6), custom_call_target="tpu_custom_call" | custom-call | flops 25769803776 | bytes 29360128 | tf_op jit(solution)/shard_map/pallas_call | solution.py:382
  453.2 1.4 copy-done.1
  455.3 1.5 pad_maximum_fusion.4
  456.8 1.3 fusion.15
  458.8 2.2 add_convert_fusion.2.x_ref
  461.0 7.8 rows_to_heads.4.dm_ref
  468.8 22.4 %attention_bwd.2 = (bf16[2,8,192,256]{3,2,1,0:T(8,128)(2,1)}, bf16[2,1536,512]{2,1,0:T(8,128)(2,1)}) custom-call(s32[7]{0:T(128)} %pad_add_fusion.1.lens_ref, bf16[3,8,192,256]{3,2,1,0:T(8,128)(2,1)} %rows_to_heads.3.q_ref, bf16[3,1536,512]{2,1,0:T(8,128)(2,1)} %all-gather.11.cloned.1.call-done.k_ref.v_ref, ...), custom_call_target="tpu_custom_call" | custom-call | flops 12079595520 | bytes 12582912 | tf_op jit(solution)/shard_map/attention_bwd/pallas_call | solution.py:291
  491.5 2.0 fusion.23
  493.5 2.8 add_convert_fusion.3.x_ref
  496.3 6.9 rows_to_heads.5.dm_ref
  503.1 13.4 %attention_bwd.3 = (bf16[1,8,192,256]{3,2,1,0:T(8,128)(2,1)}, bf16[1,1536,512]{2,1,0:T(8,128)(2,1)}) custom-call(s32[7]{0:T(128)} %pad_add_fusion.1.lens_ref, bf16[3,8,192,256]{3,2,1,0:T(8,128)(2,1)} %rows_to_heads.3.q_ref, bf16[3,1536,512]{2,1,0:T(8,128)(2,1)} %all-gather.11.cloned.1.call-done.k_ref.v_ref, ...), custom_call_target="tpu_custom_call" | custom-call | flops 6039797760 | bytes 6291456 | tf_op jit(solution)/shard_map/attention_bwd/pallas_call | solution.py:291
  518.1 1.2 constant_dynamic-update-slice_fusion.dq_ref.q_ref
  519.3 1.4 copy-done.7
  520.7 13.0 %query_weight_grad.1 = f32[8,2048,256]{2,1,0:T(8,128)} custom-call(bf16[3,192,2048]{2,1,0:T(8,128)(2,1)} %copy-done.5, bf16[3,8,192,256]{3,2,1,0:T(8,128)(2,1)} %copy-done.7), custom_call_target="tpu_custom_call" | custom-call | flops 4831838208 | bytes 16777216 | tf_op jit(solution)/shard_map/query_weight_grad/pallas_call | solution.py:170
  533.7 49.0 %mlp_out.1 = (bf16[4,3,192,2048]{3,2,1,0:T(8,128)(2,1)}, bf16[4,3,192,2048]{3,2,1,0:T(8,128)(2,1)}) custom-call(s32[1]{0:T(128)} %bitcast.9.core_ref, bf16[1536,2048]{1,0:T(8,128)(2,1)} %get-tuple-element.81.refs_0_, bf16[1536,2048]{1,0:T(8,128)(2,1)} %get-tuple-element.82.refs_1_, bf16[1536,2048]{1,0:T(8,128)(2,1)} %get-tuple-element.83.refs_2_, ...), custom_call_target="tpu_custom_call" | custom-call | flops 38654705664 | bytes 37748736 | tf_op jit(solution)/shard_map/mlp_out/pallas_call | solution.py:415
  582.8 1.3 pad_maximum_fusion.6
  584.3 0.9 pad_maximum_fusion.7.kv_ref
  585.1 3.9 convolution_bitcast_fusion
  589.0 11.3 %input_grad.1 = bf16[3,192,2048]{2,1,0:T(8,128)(2,1)} custom-call(bf16[3,8,192,256]{3,2,1,0:T(8,128)(2,1)} %copy-done.7, bf16[3,192,512]{2,1,0:T(8,128)(2,1)} %pad_maximum_fusion.7.kv_ref, bf16[8,2,256,2048]{3,2,1,0:T(8,128)(2,1)} %bitcast.58, bf16[2048,256]{1,0:T(8,128)(2,1)} %wk_ref.1, bf16[2048,256]{1,0:T(8,128)(2,1)} %wv_ref.1), custom_call_target="tpu_custom_call" | custom-call | flops 6039797760 | bytes 8388608 | tf_op jit(solution)/shard_map/input_grad/pallas_call | solution.py:118
  600.3 3.8 fusion.11
  604.1 11.4 %concatenate.46 = f32[2112,512]{1,0:T(8,128)} concatenate(f32[2048,512]{1,0:T(8,128)} %convolution_bitcast_fusion, f32[4,512]{1,0:T(4,128)S(1)} %concatenate.45, f32[4,512]{1,0:T(4,128)S(1)} %add.202, f32[56,512]{1,0:T(8,128)S(1)} %broadcast_in_dim.72), dimensions={0} | concatenate | bytes 8650752 | tf_op jit(solution)/shard_map/concatenate | solution.py:577
  615.6 1.0 copy-done.10
  616.6 3.0 pad_maximum_fusion.d_ref
  619.6 12.3 %out_weight_grad.1 = f32[8,256,2048]{2,1,0:T(8,128)} custom-call(bf16[3,8,192,256]{3,2,1,0:T(8,128)(2,1)} %get-tuple-element.80.x_ref.mixed_ref.a_ref, bf16[3,192,2048]{2,1,0:T(8,128)(2,1)} %pad_maximum_fusion.d_ref), custom_call_target="tpu_custom_call" | custom-call | flops 4831838208 | bytes 16777216 | tf_op jit(solution)/shard_map/out_weight_grad/pallas_call | solution.py:144
  631.9 48.2 %weight_grad.3 = f32[2048,2048]{1,0:T(8,128)} custom-call(bf16[1,1536,2048]{2,1,0:T(8,128)(2,1)} %bitcast.75, bf16[1,1536,2048]{2,1,0:T(8,128)(2,1)} %bitcast.77, bf16[1,1536,2048]{2,1,0:T(8,128)(2,1)} %bitcast.79, bf16[1,1536,2048]{2,1,0:T(8,128)(2,1)} %all-gather.15.cloned.1.call-done.g_ref.refs_3_, ...), custom_call_target="tpu_custom_call" | custom-call | flops 38654705664 | bytes 37748736 | tf_op jit(solution)/shard_map/weight_grad/pallas_call | solution.py:448
  680.2 47.9 %weight_grad.4 = f32[2048,2048]{1,0:T(8,128)} custom-call(bf16[1,1536,2048]{2,1,0:T(8,128)(2,1)} %all-gather.13.cloned.1.call-done.z_ref.refs_0_, bf16[1,1536,2048]{2,1,0:T(8,128)(2,1)} %all-gather.17.cloned.1.call-done.z_ref.refs_1_, bf16[1,1536,2048]{2,1,0:T(8,128)(2,1)} %all-gather.21.cloned.1.call-done.z_ref.refs_2_, bf16[1,1536,2048]{2,1,0:T(8,128)(2,1)} %bitcast.74, ...), custom_call_target="tpu_custom_call" | custom-call | flops 38654705664 | bytes 37748736 | tf_op jit(solution)/shard_map/weight_grad/pallas_call | solution.py:448
  729.6 16.6 %collective-permute-done = bf16[4,3,192,2048]{3,2,1,0:T(8,128)(2,1)} collective-permute-done((bf16[4,3,192,2048]{3,2,1,0:T(8,128)(2,1)}, bf16[4,3,192,2048]{3,2,1,0:T(8,128)(2,1)}, u32[]{:S(2)}, u32[]{:S(2)}) %collective-permute-start) | collective-permute-done | bytes 9437216 | tf_op jit(solution)/shard_map/ppermute | solution.py:465
  746.2 11.6 %add_bitcast_fusion.1 = (f32[3,192,2048]{2,1,0:T(8,128)}, f32[3,192,2048]{2,1,0:T(8,128)}, bf16[3,192,2048]{2,1,0:T(8,128)(2,1)}) fusion(bf16[4,3,192,2048]{3,2,1,0:T(8,128)(2,1)} %collective-permute-done, s32[]{:T(128)S(6)} %select_n.48, bf16[4,3,192,2048]{3,2,1,0:T(8,128)(2,1)} %get-tuple-element.76, s32[]{:T(128)S(6)} %select_n.52, s32[]{:T(128)S(6)} %select_n.50), kind=kLoop, calls=%fused_computation.34 | loop fusion | flops 11796480 | bytes 25952268 | tf_op jit(solution)/shard_map/add | solution.py:476
  757.9 3.3 fusion.36
  761.2 1.3 collective-permute-start.3
  763.3 4.8 add_convert_fusion
  768.2 1.2 copy-done.9
  769.5 32.2 %collective-permute-done.3 = bf16[3,96,2048]{2,1,0:T(8,128)(2,1)} collective-permute-done((bf16[3,96,2048]{2,1,0:T(8,128)(2,1)}, bf16[3,96,2048]{2,1,0:T(8,128)(2,1)}, u32[]{:S(2)}, u32[]{:S(2)}) %collective-permute-start.3) | collective-permute-done | bytes 1179680 | tf_op jit(solution)/shard_map/ppermute | solution.py:461
  801.7 3.3 collective-permute-done.1
  805.0 1.7 fusion.21
  806.7 1.6 pad_maximum_fusion.1
  808.2 1.6 fusion.20
  809.9 1.6 pad_maximum_fusion.2
  811.4 3.2 collective-permute-start.4
  814.7 48.2 %weight_grad.5 = f32[2048,2048]{1,0:T(8,128)} custom-call(bf16[1,1536,2048]{2,1,0:T(8,128)(2,1)} %all-gather.13.cloned.1.call-done.z_ref.refs_0_, bf16[1,1536,2048]{2,1,0:T(8,128)(2,1)} %all-gather.17.cloned.1.call-done.z_ref.refs_1_, bf16[1,1536,2048]{2,1,0:T(8,128)(2,1)} %all-gather.21.cloned.1.call-done.z_ref.refs_2_, bf16[1,1536,2048]{2,1,0:T(8,128)(2,1)} %bitcast.71, ...), custom_call_target="tpu_custom_call" | custom-call | flops 38654705664 | bytes 37748736 | tf_op jit(solution)/shard_map/weight_grad/pallas_call | solution.py:448
  862.9 25.3 %collective-permute-done.2 = bf16[3,192,2048]{2,1,0:T(8,128)(2,1)} collective-permute-done((bf16[3,192,2048]{2,1,0:T(8,128)(2,1)}, bf16[3,192,2048]{2,1,0:T(8,128)(2,1)}, u32[]{:S(2)}, u32[]{:S(2)}) %collective-permute-start.2) | collective-permute-done | bytes 2359328 | tf_op jit(solution)/shard_map/ppermute | solution.py:461
  888.3 2.1 collective-permute-done.4
  890.4 8.2 fusion.7
  900.6 4.6 fusion.35
  905.2 17.3 %reduce-scatter.21.cloned.1.call-done = f32[1,2048,256]{2,1,0:T(8,128)} async-done(((f32[8,2048,256]{2,1,0:T(8,128)}), f32[1,2048,256]{2,1,0:T(8,128)}) %reduce-scatter.21.cloned.1.call-update) | async-done | bytes 2097168 | tf_op jit(solution)/shard_map/reduce_scatter | solution.py:498
  922.5 89.5 %reduce-scatter.23.cloned.1.call-done = f32[1,256,2048]{2,1,0:T(8,128)} async-done(((f32[8,256,2048]{2,1,0:T(8,128)}), f32[1,256,2048]{2,1,0:T(8,128)}) %reduce-scatter.23.cloned.1.call-update) | async-done | bytes 2097168 | tf_op jit(solution)/shard_map/reduce_scatter | solution.py:498
  (142 shorter events, 20.5 us)
Async XLA Ops:
  7.2 88.4 %all-gather.27.cloned.1.call-start = ((), (), s32[]{:S(2)}) async-start(), calls=%async_computation.24 | async-start | bytes 18874368 | tf_op jit(solution)/shard_map/all_gather | solution.py:490
  8.8 3.1 copy-start.3
  11.7 0.7 copy-start.27
  11.7 116.8 %all-gather.11.cloned.1.call-start = ((), (), s32[]{:S(2)}) async-start(), calls=%async_computation.8 | async-start | bytes 5308416 | tf_op jit(solution)/shard_map/all_gather | solution.py:490
  12.4 0.6 copy-start.25
  12.4 2.2 copy-start.23
  13.0 1.7 copy-start.21
  14.0 2.1 copy-start.12
  14.0 2.1 copy-start.17
  14.0 1.3 copy-start.16
  15.3 1.4 copy-start.5
  15.3 2.0 copy-start.15
  19.0 3.8 copy-start.29
  19.0 3.8 copy-start.30
  19.0 4.6 copy-start.28
  19.1 152.5 %all-gather.15.cloned.1.call-start = ((), (), s32[]{:S(2)}) async-start(), calls=%async_computation.10 | async-start | bytes 7077888 | tf_op jit(solution)/shard_map/all_gather | solution.py:490
  22.6 183.7 %all-gather.13.cloned.1.call-start = ((), (), s32[]{:S(2)}) async-start(), calls=%async_computation.9 | async-start | bytes 7077888 | tf_op jit(solution)/shard_map/all_gather | solution.py:490
  23.6 141.7 %copy-start.19 = (f32[2048]{0:T(1024)}, f32[2048]{0:T(1024)S(1)}, u32[]{:S(2)}) copy-start(f32[2048]{0:T(1024)S(1)} %convert_add_fusion.2) | copy-start | bytes 24580
  165.4 1.4 copy-start
  168.3 119.6 %all-gather.17.cloned.1.call-start = ((), (), s32[]{:S(2)}) async-start(), calls=%async_computation.11 | async-start | bytes 7077888 | tf_op jit(solution)/shard_map/all_gather | solution.py:490
  169.0 118.9 %all-gather.19.cloned.1.call-start = ((), (), s32[]{:S(2)}) async-start(), calls=%async_computation.12 | async-start | bytes 7077888 | tf_op jit(solution)/shard_map/all_gather | solution.py:490
  169.6 201.6 %all-gather.21.cloned.1.call-start = ((), (), s32[]{:S(2)}) async-start(), calls=%async_computation.13 | async-start | bytes 7077888 | tf_op jit(solution)/shard_map/all_gather | solution.py:490
  170.4 200.8 %all-gather.23.cloned.1.call-start = ((), (), s32[]{:S(2)}) async-start(), calls=%async_computation.14 | async-start | bytes 7077888 | tf_op jit(solution)/shard_map/all_gather | solution.py:490
  171.2 284.0 %reduce-scatter.11.cloned.1.call-start = ((), (), s32[]{:S(2)}) async-start(), calls=%async_computation.16 | async-start | bytes 7077888 | tf_op jit(solution)/shard_map/reduce_scatter | solution.py:498
  287.5 167.7 %reduce-scatter.13.cloned.1.call-start = ((), (), s32[]{:S(2)}) async-start(), calls=%async_computation.17 | async-start | bytes 7077888 | tf_op jit(solution)/shard_map/reduce_scatter | solution.py:498
  370.6 120.9 %reduce-scatter.9.cloned.1.call-start = ((), (), s32[]{:S(2)}) async-start(), calls=%async_computation.15 | async-start | bytes 7077888 | tf_op jit(solution)/shard_map/reduce_scatter | solution.py:498
  452.9 1.7 copy-start.1
  453.0 129.8 %reduce-scatter.17.cloned.1.call-start = ((), (), s32[]{:S(2)}) async-start(), calls=%async_computation.19 | async-start | bytes 1769472 | tf_op jit(solution)/shard_map/reduce_scatter | solution.py:498
  454.8 2.0 copy-start.20
  456.8 2.0 copy-start.11
  516.5 1.4 copy-start.14
  516.6 66.2 %reduce-scatter.15.cloned.1.call-start = ((), (), s32[]{:S(2)}) async-start(), calls=%async_computation.18 | async-start | bytes 3538944 | tf_op jit(solution)/shard_map/reduce_scatter | solution.py:498
  517.4 210.7 %reduce-scatter.19.cloned.1.call-start = ((), (), s32[]{:S(2)}) async-start(), calls=%async_computation.20 | async-start | bytes 4866048 | tf_op jit(solution)/shard_map/reduce_scatter | solution.py:498
  519.3 1.4 copy-start.7
  582.7 1.4 copy-start.13
  582.7 1.5 copy-start.18
  582.7 2.4 copy-start.6
  589.0 11.3 %copy-start.4 = (bf16[3,192,2048]{2,1,0:T(8,128)(2,1)S(1)}, bf16[3,192,2048]{2,1,0:T(8,128)(2,1)}, u32[]{:S(2)}) copy-start(bf16[3,192,2048]{2,1,0:T(8,128)(2,1)} %param.13) | copy-start | bytes 7077892
  589.0 11.3 %copy-start.22 = (f32[2048]{0:T(1024)S(1)}, f32[2048]{0:T(1024)}, u32[]{:S(2)}) copy-start(f32[2048]{0:T(1024)} %copy-done.21) | copy-start | bytes 24580
  589.0 11.3 %copy-start.24 = (f32[3,192]{1,0:T(4,128)S(1)}, f32[3,192]{1,0:T(4,128)}, u32[]{:S(2)}) copy-start(f32[3,192]{1,0:T(4,128)} %copy-done.23) | copy-start | bytes 6916
  615.5 1.1 copy-start.10
  615.5 283.1 %all-gather.25.cloned.1.call-start = ((), (), s32[]{:S(2)}) async-start(), calls=%async_computation.21 | async-start | bytes 4866048 | tf_op jit(solution)/shard_map/all_gather | solution.py:490
  728.1 194.3 %reduce-scatter.21.cloned.1.call-start = ((), (), s32[]{:S(2)}) async-start(), calls=%async_computation.22 | async-start | bytes 18874368 | tf_op jit(solution)/shard_map/reduce_scatter | solution.py:498
  728.8 283.2 %reduce-scatter.23.cloned.1.call-start = ((), (), s32[]{:S(2)}) async-start(), calls=%async_computation.23 | async-start | bytes 18874368 | tf_op jit(solution)/shard_map/reduce_scatter | solution.py:498
  729.4 16.8 %collective-permute-start = (bf16[4,3,192,2048]{3,2,1,0:T(8,128)(2,1)}, bf16[4,3,192,2048]{3,2,1,0:T(8,128)(2,1)}, u32[]{:S(2)}, u32[]{:S(2)}) collective-permute-start(bf16[4,3,192,2048]{3,2,1,0:T(8,128)(2,1)} %get-tuple-element.77), channel_id=1, source_target_pairs={{0,1},{1,0},{2,3},{3,2},{4,5},{5,4},{6,7},{7,6},{8,9},{9,8},{10,11... | collective-permute-start | bytes 28311560 | tf_op jit(solution)/shard_map/ppermute | solution.py:465
  757.9 5.3 copy-start.26
  761.2 40.5 %collective-permute-start.3 = (bf16[3,96,2048]{2,1,0:T(8,128)(2,1)}, bf16[3,96,2048]{2,1,0:T(8,128)(2,1)}, u32[]{:S(2)}, u32[]{:S(2)}) collective-permute-start(bf16[3,96,2048]{2,1,0:T(8,128)(2,1)} %get-tuple-element.111), channel_id=1, source_target_pairs={{0,6},{1,7},{2,0},{3,1},{4,2},{5,3},{6,4},{7,5},{8,14},{9,15},{10,... | collective-permute-start | bytes 3538952 | tf_op jit(solution)/shard_map/ppermute | solution.py:461
  762.5 42.5 %collective-permute-start.1 = (bf16[3,96,2048]{2,1,0:T(8,128)(2,1)}, bf16[3,96,2048]{2,1,0:T(8,128)(2,1)}, u32[]{:S(2)}, u32[]{:S(2)}) collective-permute-start(bf16[3,96,2048]{2,1,0:T(8,128)(2,1)} %get-tuple-element.110), channel_id=1, source_target_pairs={{0,2},{1,3},{2,4},{3,5},{4,6},{5,7},{6,0},{7,1},{8,10},{9,11},{10,... | collective-permute-start | bytes 3538952 | tf_op jit(solution)/shard_map/ppermute | solution.py:461
  763.2 4.8 copy-start.8
  763.2 6.1 copy-start.9
  808.2 80.0 %collective-permute-start.2 = (bf16[3,192,2048]{2,1,0:T(8,128)(2,1)}, bf16[3,192,2048]{2,1,0:T(8,128)(2,1)}, u32[]{:S(2)}, u32[]{:S(2)}) collective-permute-start(bf16[3,192,2048]{2,1,0:T(8,128)(2,1)} %pad_maximum_fusion.1), channel_id=1, source_target_pairs={{0,2},{1,3},{2,4},{3,5},{4,6},{5,7},{6,0},{7,1},{8,10},{9,11},{10,... | collective-permute-start | bytes 7077896 | tf_op jit(solution)/shard_map/ppermute | solution.py:461
  811.4 78.9 %collective-permute-start.4 = (bf16[3,192,2048]{2,1,0:T(8,128)(2,1)}, bf16[3,192,2048]{2,1,0:T(8,128)(2,1)}, u32[]{:S(2)}, u32[]{:S(2)}) collective-permute-start(bf16[3,192,2048]{2,1,0:T(8,128)(2,1)} %pad_maximum_fusion.2), channel_id=1, source_target_pairs={{0,6},{1,7},{2,0},{3,1},{4,2},{5,3},{6,4},{7,5},{8,14},{9,15},{10,... | collective-permute-start | bytes 7077896 | tf_op jit(solution)/shard_map/ppermute | solution.py:461
  814.7 75.7 %copy-start.2 = (bf16[3,192,2048]{2,1,0:T(8,128)(2,1)S(1)}, bf16[3,192,2048]{2,1,0:T(8,128)(2,1)}, u32[]{:S(2)}) copy-start(bf16[3,192,2048]{2,1,0:T(8,128)(2,1)} %copy-done) | copy-start | bytes 7077892
Sparse Core Ops, SparseCore 0:
  11.8 83.6 all-gather.26
  97.7 30.7 all-gather.10
  130.7 36.7 all-gather.14
  169.4 36.8 all-gather.12
  208.3 36.8 all-gather.16
  246.6 36.8 all-gather.18
  285.6 36.8 all-gather.20
  324.5 36.8 all-gather.22
  364.3 38.4 reduce-scatter.10
  405.5 38.1 reduce-scatter.12
  453.1 38.3 reduce-scatter.8
  516.7 28.5 reduce-scatter.16
  548.2 30.7 reduce-scatter.14
  615.6 33.7 reduce-scatter.18
  728.3 28.0 all-gather.24
  759.1 163.3 reduce-scatter.20
  925.3 86.7 reduce-scatter.22

commit v2 on v1

--- a/solution.py
+++ b/solution.py
@@ -48,72 +48,69 @@
     return pl.CostEstimate(flops=int(flops), bytes_accessed=int(nbytes), transcendentals=0)
 
 
-def rows_to_heads(x_in, weights, plane, group, tables=None):
+def slot_specs(slots, width, tile, column):
+    return [pl.BlockSpec((1, width, tile), lambda *ids, k=k: (k, 0, column(*ids))) for _, k in slots]
+
+
+def rows_to_heads(x_in, slots, width, tables=None):
     batch, rows, depth = x_in.shape
-    heads, _, width, _ = weights.shape
-
-    def kernel(x_ref, w_ref, *refs):
+    heads = len(slots)
+
+    def kernel(x_ref, *refs):
         o_ref = refs[-1]
         x_all = x_ref[...].reshape(batch * rows, depth)
-        raw = dot(x_all, w_ref[...].reshape(group * width, depth), NT)
-        for n in range(group):
-            one = raw[:, n * width:(n + 1) * width].reshape(batch, rows, width)
+        for n in range(heads):
+            one = dot(x_all, refs[n][0], NT).reshape(batch, rows, width)
             if tables is not None:
-                one = rotate(one, refs[0][...], refs[1][...])
+                one = rotate(one, refs[heads][...], refs[heads + 1][...])
             o_ref[:, n] = one.astype(BF16)
 
     table_spec = pl.BlockSpec((rows, width // 2), lambda n: (0, 0))
     return pl.pallas_call(
         kernel,
         out_shape=jax.ShapeDtypeStruct((batch, heads, rows, width), BF16),
-        grid=(heads // group,),
-        in_specs=[
-            pl.BlockSpec((batch, rows, depth), lambda n: (0, 0, 0)),
-            pl.BlockSpec((group, 1, width, depth), lambda n: (n, plane, 0, 0)),
-        ] + [table_spec] * (0 if tables is None else 2),
-        out_specs=pl.BlockSpec((batch, group, rows, width), lambda n: (0, n, 0, 0)),
+        grid=(1,),
+        in_specs=[pl.BlockSpec((batch, rows, depth), lambda n: (0, 0, 0))] + slot_specs(slots, width, depth, lambda n: 0)
+        + [table_spec] * (0 if tables is None else 2),
+        out_specs=pl.BlockSpec((batch, heads, rows, width), lambda n: (0, 0, 0, 0)),
         compiler_params=params("arbitrary"),
         cost_estimate=cost(2 * batch * rows * depth * heads * width, 2 * heads * depth * width),
         name="rows_to_heads",
-    )(x_in, weights, *(() if tables is None else tables))
-
-
-def heads_to_rows(x_heads, weights, tile):
+    )(x_in, *[a for a, _ in slots], *(() if tables is None else tables))
+
+
+def heads_to_rows(x_heads, slots, depth, tile):
     batch, heads, rows, width = x_heads.shape
-    depth = weights.shape[3]
-
-    def kernel(x_ref, w_ref, o_ref):
+
+    def kernel(x_ref, *refs):
         total = None
         for n in range(heads):
-            term = dot(x_ref[:, n].reshape(batch * rows, width), w_ref[n, 0])
+            term = dot(x_ref[:, n].reshape(batch * rows, width), refs[n][0])
             total = term if total is None else total + term
-        o_ref[...] = total.reshape(batch, rows, tile)
+        refs[-1][...] = total.reshape(batch, rows, tile)
 
     return pl.pallas_call(
         kernel,
         out_shape=jax.ShapeDtypeStruct((batch, rows, depth), F32),
         grid=(depth // tile,),
-        in_specs=[
-            pl.BlockSpec((batch, heads, rows, width), lambda j: (0, 0, 0, 0)),
-            pl.BlockSpec((heads, 1, width, tile), lambda j: (0, 1, 0, j)),
-        ],
+        in_specs=[pl.BlockSpec((batch, heads, rows, width), lambda j: (0, 0, 0, 0))] + slot_specs(slots, width, tile, lambda j: j),
         out_specs=pl.BlockSpec((batch, rows, tile), lambda j: (0, 0, j)),
         compiler_params=params("arbitrary"),
         cost_estimate=cost(2 * batch * rows * depth * heads * width, 2 * heads * depth * width),
         name="heads_to_rows",
-    )(x_heads, weights)
-
-
-def input_grad(dq_heads, d_kv, weights, w_key, w_value, tile):
+    )(x_heads, *[a for a, _ in slots])
+
+
+def input_grad(dq_heads, d_kv, slots, w_key, w_value, tile):
     batch, heads, rows, width = dq_heads.shape
-    depth = weights.shape[3]
-
-    def kernel(q_ref, kv_ref, w_ref, wk_ref, wv_ref, o_ref):
+    depth = w_key.shape[0]
+
+    def kernel(q_ref, kv_ref, wk_ref, wv_ref, *refs):
         kv_all = kv_ref[...].reshape(batch * rows, 2 * width)
         total = dot(kv_all[:, :width], wk_ref[...], NT) + dot(kv_all[:, width:], wv_ref[...], NT)
         for n in range(heads):
-            total = total + dot(q_ref[:, n].reshape(batch * rows, width), w_ref[n, 0])
-        o_ref[...] = total.reshape(batch, rows, tile).astype(BF16)
+            total = total + dot(q_ref[:, n].reshape(batch * rows, width), refs[n][0])
+        refs[-1][...] = total.reshape(batch, rows, tile).astype(BF16)
 
     return pl.pallas_call(
         kernel,
@@ -122,45 +119,47 @@
         in_specs=[
             pl.BlockSpec((batch, heads, rows, width), lambda j: (0, 0, 0, 0)),
             pl.BlockSpec((batch, rows, 2 * width), lambda j: (0, 0, 0)),
-            pl.BlockSpec((heads, 1, width, tile), lambda j: (0, 0, 0, j)),
             pl.BlockSpec((tile, width), lambda j: (j, 0)),
             pl.BlockSpec((tile, width), lambda j: (j, 0)),
-        ],
+        ] + slot_specs(slots, width, tile, lambda j: j),
         out_specs=pl.BlockSpec((batch, rows, tile), lambda j: (0, 0, j)),
         compiler_params=params("arbitrary"),
         cost_estimate=cost(2 * batch * rows * depth * (heads + 2) * width, 2 * heads * depth * width),
         name="input_grad",
-    )(dq_heads, d_kv, weights, w_key, w_value)
-
-
-def out_weight_grad(mixed, d_rows):
+    )(dq_heads, d_kv, w_key, w_value, *[a for a, _ in slots])
+
+
+def out_weight_grad(mixed, d_rows, ranks):
     batch, heads, rows, width = mixed.shape
     depth = d_rows.shape[2]
 
-    def kernel(a_ref, d_ref, o_ref):
+    def kernel(rank_ref, a_ref, d_ref, o_ref):
         left = a_ref[:, 0].reshape(batch * rows, width).T
         o_ref[0] = dot(left, d_ref[...].reshape(batch * rows, depth))
 
     return pl.pallas_call(
         kernel,
         out_shape=jax.ShapeDtypeStruct((heads, width, depth), F32),
-        grid=(heads,),
-        in_specs=[
-            pl.BlockSpec((batch, 1, rows, width), lambda n: (0, n, 0, 0)),
-            pl.BlockSpec((batch, rows, depth), lambda n: (0, 0, 0)),
-        ],
-        out_specs=pl.BlockSpec((1, width, depth), lambda n: (n, 0, 0)),
+        grid_spec=pltpu.PrefetchScalarGridSpec(
+            num_scalar_prefetch=1,
+            grid=(heads,),
+            in_specs=[
+                pl.BlockSpec((batch, 1, rows, width), lambda n, s: (0, n, 0, 0)),
+                pl.BlockSpec((batch, rows, depth), lambda n, s: (0, 0, 0)),
+            ],
+            out_specs=pl.BlockSpec((1, width, depth), lambda n, s: (s[n], 0, 0)),
+        ),
         compiler_params=params("arbitrary"),
         cost_estimate=cost(2 * batch * rows * depth * heads * width, 4 * heads * depth * width),
         name="out_weight_grad",
-    )(mixed, d_rows)
-
-
-def query_weight_grad(normed, dq_heads):
+    )(ranks, mixed, d_rows)
+
+
+def query_weight_grad(normed, dq_heads, ranks):
     batch, heads, rows, width = dq_heads.shape
     depth = normed.shape[2]
 
-    def kernel(u_ref, dq_ref, o_ref, ut_ref):
+    def kernel(rank_ref, u_ref, dq_ref, o_ref, ut_ref):
         @pl.when(pl.program_id(0) == 0)
         def _():
             ut_ref[...] = u_ref[...].reshape(batch * rows, depth).T
@@ -170,17 +169,38 @@
     return pl.pallas_call(
         kernel,
         out_shape=jax.ShapeDtypeStruct((heads, depth, width), F32),
-        grid=(heads,),
-        in_specs=[
-            pl.BlockSpec((batch, rows, depth), lambda n: (0, 0, 0)),
-            pl.BlockSpec((batch, 1, rows, width), lambda n: (0, n, 0, 0)),
-        ],
-        out_specs=pl.BlockSpec((1, depth, width), lambda n: (n, 0, 0)),
-        scratch_shapes=[pltpu.VMEM((depth, batch * rows), BF16)],
+        grid_spec=pltpu.PrefetchScalarGridSpec(
+            num_scalar_prefetch=1,
+            grid=(heads,),
+            in_specs=[
+                pl.BlockSpec((batch, rows, depth), lambda n, s: (0, 0, 0)),
+                pl.BlockSpec((batch, 1, rows, width), lambda n, s: (0, n, 0, 0)),
+            ],
+            out_specs=pl.BlockSpec((1, depth, width), lambda n, s: (s[n], 0, 0)),
+            scratch_shapes=[pltpu.VMEM((depth, batch * rows), BF16)],
+        ),
         compiler_params=params("arbitrary"),
         cost_estimate=cost(2 * batch * rows * depth * heads * width, 4 * heads * depth * width),
         name="query_weight_grad",
-    )(normed, dq_heads)
+    )(ranks, normed, dq_heads)
+
+
+def small_grads(normed, d_kv, norms):
+    batch, rows, depth = normed.shape
+    width = d_kv.shape[2]
+    extra = norms.shape[0]
+
+    def kernel(u_ref, kv_ref, norm_ref, o_ref):
+        o_ref[:depth] = dot(u_ref[...].reshape(batch * rows, depth), kv_ref[...].reshape(batch * rows, width), TN)
+        o_ref[depth:] = norm_ref[...]
+
+    return pl.pallas_call(
+        kernel,
+        out_shape=jax.ShapeDtypeStruct((depth + extra, width), F32),
+        compiler_params=pltpu.CompilerParams(vmem_limit_bytes=VMEM_LIMIT),
+        cost_estimate=cost(2 * batch * rows * depth * width, 4 * depth * width),
+        name="small_grads",
+    )(normed, d_kv, norms)
 
 
 def fill_bias(lens_ref, bias_ref, rows, c):
@@ -192,8 +212,8 @@
     bias_ref[...] = jnp.where(visible, 0.0, -1e30).astype(F32)
 
 
-def attention_fwd(q_heads, keys_values, lens, group, block):
-    batch, heads, rows, width = q_heads.shape
+def attention_fwd(q_heads, keys_values, lens, group, block, start, batch):
+    _, heads, rows, width = q_heads.shape
     length = keys_values.shape[1]
     cols = group * rows
     scale = width ** -0.5
@@ -203,7 +223,7 @@
 
         @pl.when(g == 0)
         def _():
-            fill_bias(lens_ref, bias_ref, rows, c)
+            fill_bias(lens_ref, bias_ref, rows, c + start)
             vt_ref[...] = v_ref[0].T
 
         q_s = q_ref[0].reshape(cols, width) * jnp.asarray(scale, BF16)
@@ -235,9 +255,9 @@
             num_scalar_prefetch=1,
             grid=(batch, heads // group),
             in_specs=[
-                pl.BlockSpec((1, group, rows, width), lambda c, g, s: (c, g, 0, 0)),
-                pl.BlockSpec((1, length, width), lambda c, g, s: (c, 0, 0)),
-                pl.BlockSpec((1, length, width), lambda c, g, s: (c, 0, 1)),
+                pl.BlockSpec((1, group, rows, width), lambda c, g, s: (c + start, g, 0, 0)),
+                pl.BlockSpec((1, length, width), lambda c, g, s: (c + start, 0, 0)),
+                pl.BlockSpec((1, length, width), lambda c, g, s: (c + start, 0, 1)),
             ],
             out_specs=(
                 pl.BlockSpec((1, group, rows, width), lambda c, g, s: (c, g, 0, 0)),
@@ -465,6 +485,26 @@
     return lax.ppermute(x_in, "tp", [(t, t ^ 1) for t in range(size)])
 
 
+def share_weights(pair, me, size):
+    chip, core = me // 2, me % 2
+    behind, ahead = chip_shift(pair, 1, size), chip_shift(pair, -1, size)
+    far = (chip_shift(behind[:1], 1, size), chip_shift(ahead[1:], -1, size))
+    near = [(piece, swap_cores(piece, size)) for piece in (pair, behind, ahead)]
+    far = [(piece, swap_cores(piece, size)) for piece in far]
+    slots = ([], [])
+    for pieces in near:
+        for piece in pieces:
+            slots[0].append((piece, 0))
+            slots[1].append((piece, 1))
+    for plane in (0, 1):
+        slots[plane].extend((piece, 0) for piece in far[plane])
+    ranks = []
+    for back in (0, -1, 1, 2):
+        source = 2 * ((chip + back) % (size // 2))
+        ranks += [source + core, source + 1 - core]
+    return slots[0], slots[1], jnp.stack(ranks).astype(jnp.int32)
+
+
 def scatter_by_sends(keep, arrived, chip, size, marks):
     chips, count, shard, depth = keep.shape
     half = shard // 2
@@ -512,24 +552,31 @@
         cos_t, sin_t = rope_tables(first + jnp.arange(shard_len), head_dim)
         lens = jnp.concatenate([first[None].astype(jnp.int32), jnp.stack([prefix_len, valid_len], axis=1).reshape(-1).astype(jnp.int32)])
 
-        weights = gather(jnp.stack([w_query.T, w_out])[None], 0)
+        me = lax.axis_index("tp")
+        chip, core = me // 2, me % 2
+        wq_slots, wo_slots, ranks = share_weights(jnp.stack([w_query.T, w_out]), me, tp_size)
         normed, norm1_pull = jax.vjp(rms_norm, hidden, attn_norm.astype(F32))
         k_raw = jnp.einsum("bsd,de->bse", normed, w_key, preferred_element_type=F32)
         keys = rotate(k_raw, cos_t, sin_t).astype(BF16)
         values = jnp.einsum("bsd,de->bse", normed, w_value, preferred_element_type=F32).astype(BF16)
         keys_values = gather(jnp.concatenate([keys, values], axis=-1), 1)
-        query = rows_to_heads(normed, weights, 0, 2, (cos_t, sin_t))
-        mixed, lse = attention_fwd(query, keys_values, lens, 4, 512)
-        attn_out = heads_to_rows(mixed, weights, 1024)
-        resid = (hidden.astype(F32) + attn_out).astype(BF16)
-        gated_in = rms_norm(resid, mlp_norm.astype(F32))
-
-        me = lax.axis_index("tp")
-        chip, core = me // 2, me % 2
+        query = rows_to_heads(normed, wq_slots, head_dim, (cos_t, sin_t))
+        parts = []
+        queue = query
+        for start, stop in ((0, 1), (1, batch)):
+            mixed, lse = attention_fwd(queue, keys_values, lens, 4, 512, start, stop - start)
+            attn_out = heads_to_rows(mixed, wo_slots, model_dim, 1024)
+            resid = (hidden[start:stop].astype(F32) + attn_out).astype(BF16)
+            gated_in = rms_norm(resid, mlp_norm.astype(F32))
+            parts.append((mixed, lse, resid, gated_in))
+            queue = after(query, gated_in)
+        gated_parts = [parts[0][3]] + [parts[1][3][c:c + 1] for c in range(batch - 1)]
+        mixed, lse, resid = (jnp.concatenate([p[i] for p in parts], axis=0) for i in range(3))
+
         z_all, g_all, acts, d_gates, d_ups, d_gated = [], [], [], [], [], []
         for c in range(batch):
             g_c = (gather(grad_out[c:c + 1], 1), 0)
-            z_c = (gather(gated_in[c:c + 1], 1), 0)
+            z_c = (gather(gated_parts[c], 1), 0)
             if c:
                 z_c = (after(z_c[0], d_z_part), 0)
             act, d_gate, d_up = mlp_core(z_c, g_c, w_gate, w_up, w_down, 768, 512)
@@ -547,7 +594,7 @@
             _, norm2_pull = jax.vjp(rms_norm, resid[start:stop], mlp_norm.astype(F32))
             d_resid_norm, norm_part = norm2_pull(after(jnp.stack(d_gated[start:stop]), previous))
             d_resid = (grad_out[start:stop].astype(F32) + d_resid_norm.astype(F32)).astype(BF16)
-            d_mixed = rows_to_heads(d_resid, weights, 1, 2)
+            d_mixed = rows_to_heads(d_resid, wo_slots, head_dim)
             dq_part, d_kv_part = attention_bwd(query, keys_values, mixed, d_mixed, lse, cos_t, sin_t, lens, 4, 512, start)
             d_kv_sums.append(scatter(d_kv_part, 1))
             previous = d_kv_part
@@ -559,24 +606,23 @@
         dq_raw = jnp.concatenate(dq_parts, axis=0)
         d_kv = jnp.concatenate(d_kv_sums, axis=0)
 
-        g_query_part = query_weight_grad(after(normed, d_kv_part), dq_raw)
+        g_query_part = query_weight_grad(after(normed, d_kv_part), dq_raw, ranks)
         g_query = scatter(g_query_part, 0)[0]
         keep, send = split_product(after(acts, g_query_part), w_down, core, tp_size // 2, 768, 1024)
         arrived = swap_cores(send, tp_size)
         d_kv = after(d_kv, keep)
         d_k_raw = rotate(d_kv[..., :head_dim].astype(F32), cos_t, -sin_t).astype(BF16)
         d_kv_raw = jnp.concatenate([d_k_raw, d_kv[..., head_dim:]], axis=-1)
-        d_normed = input_grad(dq_raw, d_kv_raw, weights, w_key, w_value, 1024)
+        d_normed = input_grad(dq_raw, d_kv_raw, wq_slots, w_key, w_value, 1024)
         d_hidden_norm, g_attn_norm_part = norm1_pull(d_normed)
         grad_hidden = (d_resid.astype(F32) + d_hidden_norm.astype(F32)).astype(BF16)
 
-        g_kv_part = jnp.einsum("bsd,bse->de", normed, d_kv_raw, preferred_element_type=F32)
         norms = jnp.concatenate([g_attn_norm_part, g_mlp_norm_part]).reshape(-1, 2 * head_dim)
         count = norms.shape[0]
-        fill = jnp.zeros((-(model_dim + count) % (8 * heads), 2 * head_dim), F32)
-        small_part = jnp.concatenate([g_kv_part, norms, fill], axis=0)
+        norms = jnp.pad(norms, ((0, -(model_dim + count) % (8 * heads)), (0, 0)))
+        small_part = small_grads(normed, d_kv_raw, norms)
         small = scatter(small_part, 0)
-        g_out_part = out_weight_grad(after(mixed, small_part), d_resid)
+        g_out_part = out_weight_grad(after(mixed, small_part), d_resid, ranks)
         g_out = scatter(g_out_part, 0)
 
         g_down = weight_grad(planes(after(acts, g_out_part)), g_all, 1024, 512)
@@ -584,7 +630,7 @@
         g_up = weight_grad(z_all, planes(after(d_ups, g_gate)), 1024, 512)
         mlp_sum = scatter_by_sends(keep, arrived, chip, tp_size, (small_part, g_down, g_up)).astype(BF16)
         hidden_out = (resid.astype(F32) + mlp_sum.astype(F32)).astype(BF16)
-        small = gather(after(small, g_gate), 0)
+        small = gather(after(small, g_down), 0)
         g_key, g_value = small[:model_dim, :head_dim], small[:model_dim, head_dim:]
         g_norms = small[model_dim:model_dim + count].reshape(2, model_dim)
 

time: 1020 us -> 974 us (0.955)
  waiting for transfers between devices: 322 us -> 253 us
  Pallas kernels: 569 us -> 588 us
  starting transfers between devices: 7.79 us -> 18.7 us
    all_gather x9 -> x8, waiting for transfers between devices: 130 us -> 3.15 us  [gather(): return lax.all_gather(x_loc, 'tp', axis=axis, tiled=True)]
    ppermute x4 -> x8, waiting for transfers between devices: 62.9 us -> 133 us  [chip_shift(): lax.ppermute(x_in, 'tp', [(t, (t + 2 * step) % size) for t in range(size)])]
    reduce_scatter x8, waiting for transfers between devices: 107 us -> 94.5 us  [scatter(): return lax.psum_scatter(x_part, 'tp', scatter_dimension=axis, tiled=True)]
    concatenate x1 -> x2, local copies, waits for them, and re-layouts: 11.4 us -> 0.13 us  [local_layer(): jnp.concatenate([p[i] for p in parts], axis=0)]
    pallas_call x1 -> x2, Pallas kernels: 24 us -> 26.8 us  [attention_fwd(): pl.pallas_call(kernel, out_shape=(jax.ShapeDtypeStruct((batch, heads, row...]
  transfers between devices with their start and end apart: 22 -> 30, of which waited for: 11 -> 9; matrix products, arithmetic and copies ran while one was open for 6% -> 7% of each run, Pallas kernels for 53% -> 57%
where the time goes in v2:
time: 974 us; the launch traced here: 970 us
  Pallas kernels  588 us (60%)
  waiting for transfers between devices  253 us (26%)
  other arithmetic  63.7 us (7%)
  local copies, waits for them, and re-layouts  29.1 us (3%)
  starting transfers between devices  18.7 us (2%)
  between operations  15 us (2%)
    pallas_call x3, Pallas kernels, mlp_core(): pl.pallas_call(kernel, out_shape=(out, out, out), grid=(rows // tm, width...  145 us
    pallas_call x3, Pallas kernels, weight_grad(): pl.pallas_call(kernel, out_shape=jax.ShapeDtypeStruct((depth, width), F32...  145 us
    ppermute x8, waiting for transfers between devices, chip_shift(): lax.ppermute(x_in, 'tp', [(t, (t + 2 * step) % size) for t in range(size)])  133 us
    pallas_call x3, Pallas kernels, product_sum(): pl.pallas_call(kernel, out_shape=jax.ShapeDtypeStruct((rows, width), out_...  100 us
    reduce_scatter x8, waiting for transfers between devices, scatter(): return lax.psum_scatter(x_part, 'tp', scatter_dimension=axis, tiled=True)  94.5 us
    pallas_call x1, Pallas kernels, split_product(): pl.pallas_call(kernel, out_shape=(out, out), grid_spec=pltpu.PrefetchScal...  48.9 us
    pallas_call x2, Pallas kernels, attention_bwd(): pl.pallas_call(kernel, out_shape=(jax.ShapeDtypeStruct((batch, heads, row...  35.8 us
    pallas_call x2, Pallas kernels, attention_fwd(): pl.pallas_call(kernel, out_shape=(jax.ShapeDtypeStruct((batch, heads, row...  26.8 us
  transfers between devices with their start and end apart: 30, of which 9 were waited for; matrix products, arithmetic and copies ran while one was open for 7% of the time, Pallas kernels for 57%

profile of v2, /device:TPU:112, one launch (start us, length us, event | category | flops | bytes accessed | tf_op | source)
XLA Modules:
  0.0 969.6 jit_solution(9565881203276498862)
XLA Ops:
  7.3 2.3 fusion.5
  16.5 1.4 fusion.39
  18.3 1.5 copy.27
  19.8 1.4 pad_maximum_fusion.4.refs_0_
  21.3 2.4 collective-permute-start.1
  23.7 1.6 collective-permute-start.3
  25.4 74.8 %collective-permute-done.1.refs_2_ = bf16[2,256,2048]{2,1,0:T(8,128)(2,1)} collective-permute-done((bf16[2,256,2048]{2,1,0:T(8,128)(2,1)S(1)}, bf16[2,256,2048]{2,1,0:T(8,128)(2,1)}, u32[]{:S(2)}, u32[]{:S(2)}) %collective-permute-start.1) | collective-permute-done | bytes 2097184 | tf_op jit(solution)/shard_map/ppermute | solution.py:481
  101.5 1.7 collective-permute-start.5
  105.0 2.3 collective-permute-start.7
  107.3 30.5 %collective-permute-done.5.refs_6_ = bf16[1,256,2048]{2,1,0:T(8,128)(2,1)} collective-permute-done((bf16[1,256,2048]{2,1,0:T(8,128)(2,1)S(1)}, bf16[1,256,2048]{2,1,0:T(8,128)(2,1)}, u32[]{:S(2)}, u32[]{:S(2)}) %collective-permute-start.5) | collective-permute-done | bytes 1048608 | tf_op jit(solution)/shard_map/ppermute | solution.py:481
  139.2 1.7 collective-permute-done.6.refs_7_
  140.8 10.6 %rows_to_heads.3.q_ref = bf16[3,8,192,256]{3,2,1,0:T(8,128)(2,1)} custom-call(bf16[3,192,2048]{2,1,0:T(8,128)(2,1)} %copy-done.4, bf16[2,256,2048]{2,1,0:T(8,128)(2,1)} %copy-done, bf16[2,256,2048]{2,1,0:T(8,128)(2,1)} %collective-permute-done.refs_1_, bf16[2,256,2048]{2,1,0:T(8,128)(2,1)} %collective-permute-done.1.refs_2_, ...), custom_call_target="tpu_custom_call" | custom-call | flops 4831838208 | bytes 8388608 | tf_op jit(solution)/shard_map/rows_to_heads/pallas_call | solution.py:69
  151.4 9.9 %attention_fwd.2 = (bf16[1,8,192,256]{3,2,1,0:T(8,128)(2,1)}, f32[1,1,1536]{2,1,0:T(1,128)}) custom-call(s32[7]{0:T(128)} %pad_add_fusion.1.lens_ref, bf16[3,8,192,256]{3,2,1,0:T(8,128)(2,1)} %rows_to_heads.3.q_ref, bf16[3,1536,512]{2,1,0:T(8,128)(2,1)} %all-gather.9.cloned.1.call-done.k_ref.v_ref, bf16[3,1536,512]{2,1,0:T(8,128)(2,1)} %all-gather.9.cloned.1.call-done.k_ref.v_ref), custom_call_target="tpu_custom_call" | custom-call | flops 2415919104 | bytes 6291456 | tf_op jit(solution)/shard_map/attention_fwd/pallas_call | solution.py:248
  161.3 6.1 heads_to_rows.2
  167.4 1.7 fusion.21
  171.0 17.0 %attention_fwd.3 = (bf16[2,8,192,256]{3,2,1,0:T(8,128)(2,1)}, f32[2,1,1536]{2,1,0:T(1,128)}) custom-call(s32[7]{0:T(128)} %pad_add_fusion.1.lens_ref, bf16[3,8,192,256]{3,2,1,0:T(8,128)(2,1)} %rows_to_heads.3.q_ref, bf16[3,1536,512]{2,1,0:T(8,128)(2,1)} %all-gather.9.cloned.1.call-done.k_ref.v_ref, bf16[3,1536,512]{2,1,0:T(8,128)(2,1)} %all-gather.9.cloned.1.call-done.k_ref.v_ref), custom_call_target="tpu_custom_call" | custom-call | flops 4831838208 | bytes 12582912 | tf_op jit(solution)/shard_map/attention_fwd/pallas_call | solution.py:248
  188.0 8.3 heads_to_rows.3
  196.3 2.5 fusion.10
  198.9 2.4 fusion.15
  205.0 3.1 all-gather.11.cloned.1.call-done.z_ref.refs_0_
  208.1 47.9 %mlp_core.3 = (bf16[1536,2048]{1,0:T(8,128)(2,1)}, bf16[1536,2048]{1,0:T(8,128)(2,1)}, bf16[1536,2048]{1,0:T(8,128)(2,1)}) custom-call(bf16[1,1536,2048]{2,1,0:T(8,128)(2,1)} %all-gather.11.cloned.1.call-done.z_ref.refs_0_, bf16[1,1536,2048]{2,1,0:T(8,128)(2,1)} %all-gather.13.cloned.1.call-done.g_ref.refs_3_, bf16[2048,2048]{1,0:T(8,128)(2,1)} %refs_2_.5, ...), custom_call_target="tpu_custom_call" | custom-call | flops 38654705664 | bytes 56623104 | tf_op jit(solution)/shard_map/mlp_core/pallas_call | solution.py:374
  255.9 33.2 %shard_map.212 = bf16[1536,2048]{1,0:T(8,128)(2,1)} custom-call(bf16[1536,2048]{1,0:T(8,128)(2,1)} %get-tuple-element.91.refs_0_, bf16[1536,2048]{1,0:T(8,128)(2,1)} %get-tuple-element.94.refs_1_, bf16[2048,2048]{1,0:T(8,128)(2,1)} %refs_2_.5, bf16[2048,2048]{1,0:T(8,128)(2,1)} %refs_3_.6), custom_call_target="tpu_custom_call" | custom-call | flops 25769803776 | bytes 29360128 | tf_op jit(solution)/shard_map/pallas_call | solution.py:402
  289.6 49.1 %mlp_core.4 = (bf16[1536,2048]{1,0:T(8,128)(2,1)}, bf16[1536,2048]{1,0:T(8,128)(2,1)}, bf16[1536,2048]{1,0:T(8,128)(2,1)}) custom-call(bf16[1,1536,2048]{2,1,0:T(8,128)(2,1)} %all-gather.15.cloned.1.call-done.z_ref.refs_1_, bf16[1,1536,2048]{2,1,0:T(8,128)(2,1)} %all-gather.17.cloned.1.call-done.g_ref.refs_4_, bf16[2048,2048]{1,0:T(8,128)(2,1)} %refs_2_.5, ...), custom_call_target="tpu_custom_call" | custom-call | flops 38654705664 | bytes 56623104 | tf_op jit(solution)/shard_map/mlp_core/pallas_call | solution.py:374
  338.7 33.5 %shard_map.213 = bf16[1536,2048]{1,0:T(8,128)(2,1)} custom-call(bf16[1536,2048]{1,0:T(8,128)(2,1)} %get-tuple-element.92.refs_0_, bf16[1536,2048]{1,0:T(8,128)(2,1)} %get-tuple-element.95.refs_1_, bf16[2048,2048]{1,0:T(8,128)(2,1)} %refs_2_.5, bf16[2048,2048]{1,0:T(8,128)(2,1)} %refs_3_.6), custom_call_target="tpu_custom_call" | custom-call | flops 25769803776 | bytes 29360128 | tf_op jit(solution)/shard_map/pallas_call | solution.py:402
  372.6 48.2 %mlp_core.5 = (bf16[1536,2048]{1,0:T(8,128)(2,1)}, bf16[1536,2048]{1,0:T(8,128)(2,1)}, bf16[1536,2048]{1,0:T(8,128)(2,1)}) custom-call(bf16[1,1536,2048]{2,1,0:T(8,128)(2,1)} %all-gather.19.cloned.1.call-done.z_ref.refs_2_, bf16[1,1536,2048]{2,1,0:T(8,128)(2,1)} %all-gather.21.cloned.1.call-done.g_ref.refs_5_, bf16[2048,2048]{1,0:T(8,128)(2,1)} %refs_2_.5, ...), custom_call_target="tpu_custom_call" | custom-call | flops 38654705664 | bytes 56623104 | tf_op jit(solution)/shard_map/mlp_core/pallas_call | solution.py:374
  420.8 33.6 %shard_map.214 = bf16[1536,2048]{1,0:T(8,128)(2,1)} custom-call(bf16[1536,2048]{1,0:T(8,128)(2,1)} %get-tuple-element.93.refs_0_, bf16[1536,2048]{1,0:T(8,128)(2,1)} %get-tuple-element.96.refs_1_, bf16[2048,2048]{1,0:T(8,128)(2,1)} %refs_2_.5, bf16[2048,2048]{1,0:T(8,128)(2,1)} %refs_3_.6), custom_call_target="tpu_custom_call" | custom-call | flops 25769803776 | bytes 29360128 | tf_op jit(solution)/shard_map/pallas_call | solution.py:402
  455.0 1.5 constant_dynamic-update-slice_fusion.1
  456.7 1.4 copy-done.19
  458.5 2.2 pad_maximum_fusion.5
  462.3 2.2 add_convert_fusion.3.x_ref
  464.5 8.6 rows_to_heads.4.dm_ref
  473.1 22.6 %attention_bwd.2 = (bf16[2,8,192,256]{3,2,1,0:T(8,128)(2,1)}, bf16[2,1536,512]{2,1,0:T(8,128)(2,1)}) custom-call(s32[7]{0:T(128)} %pad_add_fusion.1.lens_ref, bf16[3,8,192,256]{3,2,1,0:T(8,128)(2,1)} %rows_to_heads.3.q_ref, bf16[3,1536,512]{2,1,0:T(8,128)(2,1)} %all-gather.9.cloned.1.call-done.k_ref.v_ref, ...), custom_call_target="tpu_custom_call" | custom-call | flops 12079595520 | bytes 12582912 | tf_op jit(solution)/shard_map/attention_bwd/pallas_call | solution.py:311
  495.8 2.0 fusion.24
  497.8 2.8 add_convert_fusion.5.x_ref
  500.6 7.4 rows_to_heads.5.dm_ref
  508.0 13.2 %attention_bwd.3 = (bf16[1,8,192,256]{3,2,1,0:T(8,128)(2,1)}, bf16[1,1536,512]{2,1,0:T(8,128)(2,1)}) custom-call(s32[7]{0:T(128)} %pad_add_fusion.1.lens_ref, bf16[3,8,192,256]{3,2,1,0:T(8,128)(2,1)} %rows_to_heads.3.q_ref, bf16[3,1536,512]{2,1,0:T(8,128)(2,1)} %all-gather.9.cloned.1.call-done.k_ref.v_ref, ...), custom_call_target="tpu_custom_call" | custom-call | flops 6039797760 | bytes 6291456 | tf_op jit(solution)/shard_map/attention_bwd/pallas_call | solution.py:311
  524.0 1.4 copy-done.17
  525.4 14.2 %query_weight_grad.1 = f32[8,2048,256]{2,1,0:T(8,128)} custom-call(s32[8]{0:T(128)} %stack.71.rank_ref, bf16[3,192,2048]{2,1,0:T(8,128)(2,1)} %copy-done.4, bf16[3,8,192,256]{3,2,1,0:T(8,128)(2,1)} %copy-done.17), custom_call_target="tpu_custom_call" | custom-call | flops 4831838208 | bytes 16777216 | tf_op jit(solution)/shard_map/query_weight_grad/pallas_call | solution.py:169
  539.6 48.9 %mlp_out.1 = (bf16[4,3,192,2048]{3,2,1,0:T(8,128)(2,1)}, bf16[4,3,192,2048]{3,2,1,0:T(8,128)(2,1)}) custom-call(s32[1]{0:T(128)} %bitcast.8.core_ref, bf16[1536,2048]{1,0:T(8,128)(2,1)} %get-tuple-element.87.refs_0_, bf16[1536,2048]{1,0:T(8,128)(2,1)} %get-tuple-element.88.refs_1_, bf16[1536,2048]{1,0:T(8,128)(2,1)} %get-tuple-element.89.refs_2_, ...), custom_call_target="tpu_custom_call" | custom-call | flops 38654705664 | bytes 37748736 | tf_op jit(solution)/shard_map/mlp_out/pallas_call | solution.py:435
  590.8 12.0 %input_grad.1 = bf16[3,192,2048]{2,1,0:T(8,128)(2,1)} custom-call(bf16[3,8,192,256]{3,2,1,0:T(8,128)(2,1)} %copy-done.17, bf16[3,192,512]{2,1,0:T(8,128)(2,1)} %pad_maximum_fusion.8.kv_ref, bf16[2048,256]{1,0:T(8,128)(2,1)} %wk_ref.1, bf16[2048,256]{1,0:T(8,128)(2,1)} %wv_ref.1, bf16[2,256,2048]{2,1,0:T(8,128)(2,1)} %copy-done, ...), custom_call_target="tpu_custom_call" | custom-call | flops 6039797760 | bytes 8388608 | tf_op jit(solution)/shard_map/input_grad/pallas_call | solution.py:115
  602.9 3.8 fusion.6
  607.3 5.7 small_grads.1
  614.2 3.0 pad_maximum_fusion.1.d_ref
  617.2 13.1 %out_weight_grad.1 = f32[8,256,2048]{2,1,0:T(8,128)} custom-call(s32[8]{0:T(128)} %stack.71.rank_ref, bf16[3,8,192,256]{3,2,1,0:T(8,128)(2,1)} %copy-done.19, bf16[3,192,2048]{2,1,0:T(8,128)(2,1)} %pad_maximum_fusion.1.d_ref), custom_call_target="tpu_custom_call" | custom-call | flops 4831838208 | bytes 16777216 | tf_op jit(solution)/shard_map/out_weight_grad/pallas_call | solution.py:140
  630.3 48.2 %weight_grad.3 = f32[2048,2048]{1,0:T(8,128)} custom-call(bf16[1,1536,2048]{2,1,0:T(8,128)(2,1)} %bitcast.76, bf16[1,1536,2048]{2,1,0:T(8,128)(2,1)} %bitcast.77, bf16[1,1536,2048]{2,1,0:T(8,128)(2,1)} %bitcast.78, bf16[1,1536,2048]{2,1,0:T(8,128)(2,1)} %all-gather.13.cloned.1.call-done.g_ref.refs_3_, ...), custom_call_target="tpu_custom_call" | custom-call | flops 38654705664 | bytes 37748736 | tf_op jit(solution)/shard_map/weight_grad/pallas_call | solution.py:468
  680.2 16.3 %collective-permute-done.9 = bf16[4,3,192,2048]{3,2,1,0:T(8,128)(2,1)} collective-permute-done((bf16[4,3,192,2048]{3,2,1,0:T(8,128)(2,1)}, bf16[4,3,192,2048]{3,2,1,0:T(8,128)(2,1)}, u32[]{:S(2)}, u32[]{:S(2)}) %collective-permute-start.9) | collective-permute-done | bytes 9437216 | tf_op jit(solution)/shard_map/ppermute | solution.py:485
  696.5 11.6 %add_bitcast_fusion.1 = (f32[3,192,2048]{2,1,0:T(8,128)}, f32[3,192,2048]{2,1,0:T(8,128)}, bf16[3,192,2048]{2,1,0:T(8,128)(2,1)}) fusion(bf16[4,3,192,2048]{3,2,1,0:T(8,128)(2,1)} %collective-permute-done.9, s32[]{:T(128)S(6)} %select_n.61, bf16[4,3,192,2048]{3,2,1,0:T(8,128)(2,1)} %get-tuple-element.82, s32[]{:T(128)S(6)} %select_n.63, s32[]{:T(128)S(6)} %select_n.62), kind=kLoop, calls=%fused_computation.26 | loop fusion | flops 11796480 | bytes 25952268 | tf_op jit(solution)/shard_map/add | solution.py:516
  708.2 3.4 fusion.38
  712.2 2.5 collective-permute-start.12
  714.8 48.3 %weight_grad.4 = f32[2048,2048]{1,0:T(8,128)} custom-call(bf16[1,1536,2048]{2,1,0:T(8,128)(2,1)} %all-gather.11.cloned.1.call-done.z_ref.refs_0_, bf16[1,1536,2048]{2,1,0:T(8,128)(2,1)} %all-gather.15.cloned.1.call-done.z_ref.refs_1_, bf16[1,1536,2048]{2,1,0:T(8,128)(2,1)} %all-gather.19.cloned.1.call-done.z_ref.refs_2_, bf16[1,1536,2048]{2,1,0:T(8,128)(2,1)} %bitcast.73, ...), custom_call_target="tpu_custom_call" | custom-call | flops 38654705664 | bytes 37748736 | tf_op jit(solution)/shard_map/weight_grad/pallas_call | solution.py:468
  763.2 4.3 add_convert_fusion
  767.6 1.6 copy-done.10
  769.4 1.7 fusion.19
  771.1 1.7 pad_maximum_fusion.2
  772.9 1.6 fusion.18
  774.5 1.6 pad_maximum_fusion.3
  776.1 3.0 collective-permute-start.13
  779.1 48.5 %weight_grad.5 = f32[2048,2048]{1,0:T(8,128)} custom-call(bf16[1,1536,2048]{2,1,0:T(8,128)(2,1)} %all-gather.11.cloned.1.call-done.z_ref.refs_0_, bf16[1,1536,2048]{2,1,0:T(8,128)(2,1)} %all-gather.15.cloned.1.call-done.z_ref.refs_1_, bf16[1,1536,2048]{2,1,0:T(8,128)(2,1)} %all-gather.19.cloned.1.call-done.z_ref.refs_2_, bf16[1,1536,2048]{2,1,0:T(8,128)(2,1)} %bitcast.70, ...), custom_call_target="tpu_custom_call" | custom-call | flops 38654705664 | bytes 37748736 | tf_op jit(solution)/shard_map/weight_grad/pallas_call | solution.py:468
  827.6 25.5 %collective-permute-done.11 = bf16[3,192,2048]{2,1,0:T(8,128)(2,1)} collective-permute-done((bf16[3,192,2048]{2,1,0:T(8,128)(2,1)}, bf16[3,192,2048]{2,1,0:T(8,128)(2,1)}, u32[]{:S(2)}, u32[]{:S(2)}) %collective-permute-start.11) | collective-permute-done | bytes 2359328 | tf_op jit(solution)/shard_map/ppermute | solution.py:481
  853.1 2.6 collective-permute-done.13
  855.7 6.1 add_convert_fusion.1
  863.8 4.6 fusion.37
  868.4 3.2 reduce-scatter.21.cloned.1.call-done
  871.6 91.2 %reduce-scatter.23.cloned.1.call-done = f32[1,256,2048]{2,1,0:T(8,128)} async-done(((f32[8,256,2048]{2,1,0:T(8,128)}), f32[1,256,2048]{2,1,0:T(8,128)}) %reduce-scatter.23.cloned.1.call-update) | async-done | bytes 2097168 | tf_op jit(solution)/shard_map/reduce_scatter | solution.py:538
  (191 shorter events, 32.2 us)
Async XLA Ops:
  7.2 3.1 copy-start.1
  7.2 3.1 copy-start.36
  7.2 144.2 %all-gather.9.cloned.1.call-start = ((), (), s32[]{:S(2)}) async-start(), calls=%async_computation.8 | async-start | bytes 5308416 | tf_op jit(solution)/shard_map/all_gather | solution.py:530
  11.5 2.0 copy-start.42
  14.3 2.2 copy-start.15
  15.4 2.6 copy-start.20
  15.4 2.6 copy-start.23
  16.4 188.6 %all-gather.13.cloned.1.call-start = ((), (), s32[]{:S(2)}) async-start(), calls=%async_computation.10 | async-start | bytes 7077888 | tf_op jit(solution)/shard_map/all_gather | solution.py:530
  18.0 190.1 %all-gather.11.cloned.1.call-start = ((), (), s32[]{:S(2)}) async-start(), calls=%async_computation.9 | async-start | bytes 7077888 | tf_op jit(solution)/shard_map/all_gather | solution.py:530
  21.3 119.5 %copy-start = (bf16[2,256,2048]{2,1,0:T(8,128)(2,1)}, bf16[2,256,2048]{2,1,0:T(8,128)(2,1)S(1)}, u32[]{:S(2)}) copy-start(bf16[2,256,2048]{2,1,0:T(8,128)(2,1)S(1)} %pad_maximum_fusion.4.refs_0_) | copy-start | bytes 6291460
  21.3 117.0 %copy-start.39 = (s32[3]{0:T(128)S(1)}, s32[3]{0:T(128)}, u32[]{:S(2)}) copy-start(s32[3]{0:T(128)} %param.16) | copy-start | bytes 40
  21.3 117.0 %copy-start.40 = (s32[3]{0:T(128)S(1)}, s32[3]{0:T(128)}, u32[]{:S(2)}) copy-start(s32[3]{0:T(128)} %param.15) | copy-start | bytes 40
  21.3 117.8 %copy-start.37 = (bf16[2048]{0:T(1024)(128)(2,1)S(1)}, bf16[2048]{0:T(1024)(128)(2,1)}, u32[]{:S(2)}) copy-start(bf16[2048]{0:T(1024)(128)(2,1)} %param.22) | copy-start | bytes 12292
  21.3 78.8 %collective-permute-start.1 = (bf16[2,256,2048]{2,1,0:T(8,128)(2,1)S(1)}, bf16[2,256,2048]{2,1,0:T(8,128)(2,1)}, u32[]{:S(2)}, u32[]{:S(2)}) collective-permute-start(bf16[2,256,2048]{2,1,0:T(8,128)(2,1)S(1)} %pad_maximum_fusion.4.refs_0_), channel_id=1, source_target_pairs={{0,2},{1,3},{2,4},{3,5},{4,6},{5,7},{6,0},{7,1},{8,10},{9,11},{10,... | collective-permute-start | bytes 6291464 | tf_op jit(solution)/shard_map/ppermute | solution.py:481
  23.7 79.4 %collective-permute-start.3 = (bf16[2,256,2048]{2,1,0:T(8,128)(2,1)S(1)}, bf16[2,256,2048]{2,1,0:T(8,128)(2,1)}, u32[]{:S(2)}, u32[]{:S(2)}) collective-permute-start(bf16[2,256,2048]{2,1,0:T(8,128)(2,1)S(1)} %pad_maximum_fusion.4.refs_0_), channel_id=1, source_target_pairs={{0,6},{1,7},{2,0},{3,1},{4,2},{5,3},{6,4},{7,5},{8,14},{9,15},{10,... | collective-permute-start | bytes 6291464 | tf_op jit(solution)/shard_map/ppermute | solution.py:481
  25.4 113.8 %collective-permute-start = (bf16[2,256,2048]{2,1,0:T(8,128)(2,1)S(1)}, bf16[2,256,2048]{2,1,0:T(8,128)(2,1)}, u32[]{:S(2)}, u32[]{:S(2)}) collective-permute-start(bf16[2,256,2048]{2,1,0:T(8,128)(2,1)S(1)} %pad_maximum_fusion.4.refs_0_), channel_id=1, source_target_pairs={{0,1},{1,0},{2,3},{3,2},{4,5},{5,4},{6,7},{7,6},{8,9},{9,8},{10,11... | collective-permute-start | bytes 6291464 | tf_op jit(solution)/shard_map/ppermute | solution.py:485
  101.5 36.3 %collective-permute-start.5 = (bf16[1,256,2048]{2,1,0:T(8,128)(2,1)S(1)}, bf16[1,256,2048]{2,1,0:T(8,128)(2,1)}, u32[]{:S(2)}, u32[]{:S(2)}) collective-permute-start(bf16[1,256,2048]{2,1,0:T(8,128)(2,1)S(1)} %slice.120), channel_id=1, source_target_pairs={{0,2},{1,3},{2,4},{3,5},{4,6},{5,7},{6,0},{7,1},{8,10},{9,11},{10,... | collective-permute-start | bytes 3145736 | tf_op jit(solution)/shard_map/ppermute | solution.py:481
  103.1 36.0 %collective-permute-start.4 = (bf16[2,256,2048]{2,1,0:T(8,128)(2,1)}, bf16[2,256,2048]{2,1,0:T(8,128)(2,1)}, u32[]{:S(2)}, u32[]{:S(2)}) collective-permute-start(bf16[2,256,2048]{2,1,0:T(8,128)(2,1)} %collective-permute-done.3.refs_4_), channel_id=1, source_target_pairs={{0,1},{1,0},{2,3},{3,2},{4,5},{5,4},{6,7},{7,6},{8,9},{9,8},{10,11... | collective-permute-start | bytes 6291464 | tf_op jit(solution)/shard_map/ppermute | solution.py:485
  103.1 37.7 %collective-permute-start.2 = (bf16[2,256,2048]{2,1,0:T(8,128)(2,1)}, bf16[2,256,2048]{2,1,0:T(8,128)(2,1)}, u32[]{:S(2)}, u32[]{:S(2)}) collective-permute-start(bf16[2,256,2048]{2,1,0:T(8,128)(2,1)} %collective-permute-done.1.refs_2_), channel_id=1, source_target_pairs={{0,1},{1,0},{2,3},{3,2},{4,5},{5,4},{6,7},{7,6},{8,9},{9,8},{10,11... | collective-permute-start | bytes 6291464 | tf_op jit(solution)/shard_map/ppermute | solution.py:485
  105.0 32.8 %collective-permute-start.7 = (bf16[1,256,2048]{2,1,0:T(8,128)(2,1)S(1)}, bf16[1,256,2048]{2,1,0:T(8,128)(2,1)S(1)}, u32[]{:S(2)}, u32[]{:S(2)}) collective-permute-start(bf16[1,256,2048]{2,1,0:T(8,128)(2,1)S(1)} %slice.123), channel_id=1, source_target_pairs={{0,6},{1,7},{2,0},{3,1},{4,2},{5,3},{6,4},{7,5},{8,14},{9,15},{10,... | collective-permute-start | bytes 3145736 | tf_op jit(solution)/shard_map/ppermute | solution.py:481
  137.8 3.0 collective-permute-start.6
  137.8 13.6 %copy-start.8 = (bf16[1,256,2048]{2,1,0:T(8,128)(2,1)}, bf16[1,256,2048]{2,1,0:T(8,128)(2,1)S(1)}, u32[]{:S(2)}) copy-start(bf16[1,256,2048]{2,1,0:T(8,128)(2,1)S(1)} %collective-permute-done.7.refs_6_) | copy-start | bytes 3145732
  137.8 23.5 %collective-permute-start.8 = (bf16[1,256,2048]{2,1,0:T(8,128)(2,1)S(1)}, bf16[1,256,2048]{2,1,0:T(8,128)(2,1)}, u32[]{:S(2)}, u32[]{:S(2)}) collective-permute-start(bf16[1,256,2048]{2,1,0:T(8,128)(2,1)S(1)} %collective-permute-done.7.refs_6_), channel_id=1, source_target_pairs={{0,1},{1,0},{2,3},{3,2},{4,5},{5,4},{6,7},{7,6},{8,9},{9,8},{10,11... | collective-permute-start | bytes 3145736 | tf_op jit(solution)/shard_map/ppermute | solution.py:485
  139.1 59.7 %copy-start.24 = (f32[2048]{0:T(1024)}, f32[2048]{0:T(1024)S(1)}, u32[]{:S(2)}) copy-start(f32[2048]{0:T(1024)S(1)} %convert_add_fusion) | copy-start | bytes 24580
  161.3 6.1 copy-start.2
  169.2 29.7 %copy-start.13 = (bf16[1,192,2048]{2,1,0:T(8,128)(2,1)}, bf16[1,192,2048]{2,1,0:T(8,128)(2,1)S(1)}, u32[]{:S(2)}) copy-start(bf16[1,192,2048]{2,1,0:T(8,128)(2,1)S(1)} %get-tuple-element.112) | copy-start | bytes 2359300
  170.4 119.1 %all-gather.15.cloned.1.call-start = ((), (), s32[]{:S(2)}) async-start(), calls=%async_computation.11 | async-start | bytes 7077888 | tf_op jit(solution)/shard_map/all_gather | solution.py:530
  198.8 2.4 copy-start.5
  202.6 86.9 %all-gather.17.cloned.1.call-start = ((), (), s32[]{:S(2)}) async-start(), calls=%async_computation.12 | async-start | bytes 7077888 | tf_op jit(solution)/shard_map/all_gather | solution.py:530
  203.3 169.3 %all-gather.19.cloned.1.call-start = ((), (), s32[]{:S(2)}) async-start(), calls=%async_computation.13 | async-start | bytes 7077888 | tf_op jit(solution)/shard_map/all_gather | solution.py:530
  203.9 168.7 %all-gather.21.cloned.1.call-start = ((), (), s32[]{:S(2)}) async-start(), calls=%async_computation.14 | async-start | bytes 7077888 | tf_op jit(solution)/shard_map/all_gather | solution.py:530
  204.7 253.7 %reduce-scatter.11.cloned.1.call-start = ((), (), s32[]{:S(2)}) async-start(), calls=%async_computation.16 | async-start | bytes 7077888 | tf_op jit(solution)/shard_map/reduce_scatter | solution.py:538
  289.2 169.2 %reduce-scatter.13.cloned.1.call-start = ((), (), s32[]{:S(2)}) async-start(), calls=%async_computation.17 | async-start | bytes 7077888 | tf_op jit(solution)/shard_map/reduce_scatter | solution.py:538
  372.2 123.5 %reduce-scatter.9.cloned.1.call-start = ((), (), s32[]{:S(2)}) async-start(), calls=%async_computation.15 | async-start | bytes 7077888 | tf_op jit(solution)/shard_map/reduce_scatter | solution.py:538
  454.4 2.1 copy-start.18
  454.5 3.6 copy-start.6
  454.5 134.1 %reduce-scatter.17.cloned.1.call-start = ((), (), s32[]{:S(2)}) async-start(), calls=%async_computation.19 | async-start | bytes 1769472 | tf_op jit(solution)/shard_map/reduce_scatter | solution.py:538
  456.5 1.8 copy-start.33
  456.5 1.8 copy-start.35
  456.6 1.8 copy-start.34
  458.1 2.6 copy-start.11
  458.1 2.6 copy-start.25
  458.4 3.5 copy-start.38
  460.6 1.7 copy-start.16
  521.2 1.5 copy-start.22
  521.2 67.3 %reduce-scatter.15.cloned.1.call-start = ((), (), s32[]{:S(2)}) async-start(), calls=%async_computation.18 | async-start | bytes 3538944 | tf_op jit(solution)/shard_map/reduce_scatter | solution.py:538
  521.9 156.7 %reduce-scatter.19.cloned.1.call-start = ((), (), s32[]{:S(2)}) async-start(), calls=%async_computation.20 | async-start | bytes 4866048 | tf_op jit(solution)/shard_map/reduce_scatter | solution.py:538
  524.0 1.4 copy-start.17
  590.8 12.0 %copy-start.3 = (bf16[3,192,2048]{2,1,0:T(8,128)(2,1)S(1)}, bf16[3,192,2048]{2,1,0:T(8,128)(2,1)}, u32[]{:S(2)}) copy-start(bf16[3,192,2048]{2,1,0:T(8,128)(2,1)} %param.13) | copy-start | bytes 7077892
  590.8 12.0 %copy-start.28 = (f32[2048]{0:T(1024)S(1)}, f32[2048]{0:T(1024)}, u32[]{:S(2)}) copy-start(f32[2048]{0:T(1024)} %copy-done.27) | copy-start | bytes 24580
  590.8 12.0 %copy-start.30 = (f32[3,192]{1,0:T(4,128)S(1)}, f32[3,192]{1,0:T(4,128)}, u32[]{:S(2)}) copy-start(f32[3,192]{1,0:T(4,128)} %copy-done.29) | copy-start | bytes 6916
  613.1 248.7 %all-gather.23.cloned.1.call-start = ((), (), s32[]{:S(2)}) async-start(), calls=%async_computation.21 | async-start | bytes 4866048 | tf_op jit(solution)/shard_map/all_gather | solution.py:530
  678.6 193.0 %reduce-scatter.21.cloned.1.call-start = ((), (), s32[]{:S(2)}) async-start(), calls=%async_computation.22 | async-start | bytes 18874368 | tf_op jit(solution)/shard_map/reduce_scatter | solution.py:538
  679.3 283.6 %reduce-scatter.23.cloned.1.call-start = ((), (), s32[]{:S(2)}) async-start(), calls=%async_computation.23 | async-start | bytes 18874368 | tf_op jit(solution)/shard_map/reduce_scatter | solution.py:538
  679.9 16.6 %collective-permute-start.9 = (bf16[4,3,192,2048]{3,2,1,0:T(8,128)(2,1)}, bf16[4,3,192,2048]{3,2,1,0:T(8,128)(2,1)}, u32[]{:S(2)}, u32[]{:S(2)}) collective-permute-start(bf16[4,3,192,2048]{3,2,1,0:T(8,128)(2,1)} %get-tuple-element.83), channel_id=1, source_target_pairs={{0,1},{1,0},{2,3},{3,2},{4,5},{5,4},{6,7},{7,6},{8,9},{9,8},{10,11... | collective-permute-start | bytes 28311560 | tf_op jit(solution)/shard_map/ppermute | solution.py:485
  711.5 57.9 %collective-permute-start.10 = (bf16[3,96,2048]{2,1,0:T(8,128)(2,1)}, bf16[3,96,2048]{2,1,0:T(8,128)(2,1)}, u32[]{:S(2)}, u32[]{:S(2)}) collective-permute-start(bf16[3,96,2048]{2,1,0:T(8,128)(2,1)} %get-tuple-element.120), channel_id=1, source_target_pairs={{0,2},{1,3},{2,4},{3,5},{4,6},{5,7},{6,0},{7,1},{8,10},{9,11},{10,... | collective-permute-start | bytes 3538952 | tf_op jit(solution)/shard_map/ppermute | solution.py:481
  712.2 57.2 %collective-permute-start.12 = (bf16[3,96,2048]{2,1,0:T(8,128)(2,1)}, bf16[3,96,2048]{2,1,0:T(8,128)(2,1)}, u32[]{:S(2)}, u32[]{:S(2)}) collective-permute-start(bf16[3,96,2048]{2,1,0:T(8,128)(2,1)} %get-tuple-element.121), channel_id=1, source_target_pairs={{0,6},{1,7},{2,0},{3,1},{4,2},{5,3},{6,4},{7,5},{8,14},{9,15},{10,... | collective-permute-start | bytes 3538952 | tf_op jit(solution)/shard_map/ppermute | solution.py:481
  714.8 48.4 %copy-start.32 = (f32[3,192]{1,0:T(4,128)S(1)}, f32[3,192]{1,0:T(4,128)}, u32[]{:S(2)}) copy-start(f32[3,192]{1,0:T(4,128)} %copy-done.31) | copy-start | bytes 6916
  763.1 4.3 copy-start.9
  763.1 6.1 copy-start.10
  772.7 80.4 %collective-permute-start.11 = (bf16[3,192,2048]{2,1,0:T(8,128)(2,1)}, bf16[3,192,2048]{2,1,0:T(8,128)(2,1)}, u32[]{:S(2)}, u32[]{:S(2)}) collective-permute-start(bf16[3,192,2048]{2,1,0:T(8,128)(2,1)} %pad_maximum_fusion.2), channel_id=1, source_target_pairs={{0,2},{1,3},{2,4},{3,5},{4,6},{5,7},{6,0},{7,1},{8,10},{9,11},{10,... | collective-permute-start | bytes 7077896 | tf_op jit(solution)/shard_map/ppermute | solution.py:481
  776.1 79.6 %collective-permute-start.13 = (bf16[3,192,2048]{2,1,0:T(8,128)(2,1)}, bf16[3,192,2048]{2,1,0:T(8,128)(2,1)}, u32[]{:S(2)}, u32[]{:S(2)}) collective-permute-start(bf16[3,192,2048]{2,1,0:T(8,128)(2,1)} %pad_maximum_fusion.3), channel_id=1, source_target_pairs={{0,6},{1,7},{2,0},{3,1},{4,2},{5,3},{6,4},{7,5},{8,14},{9,15},{10,... | collective-permute-start | bytes 7077896 | tf_op jit(solution)/shard_map/ppermute | solution.py:481
  779.1 76.6 %copy-start.7 = (bf16[2,192,2048]{2,1,0:T(8,128)(2,1)S(1)}, bf16[2,192,2048]{2,1,0:T(8,128)(2,1)}, u32[]{:S(2)}) copy-start(bf16[2,192,2048]{2,1,0:T(8,128)(2,1)} %copy-done.5) | copy-start | bytes 4718596
  779.1 76.6 %copy-start.14 = (bf16[1,192,2048]{2,1,0:T(8,128)(2,1)S(1)}, bf16[1,192,2048]{2,1,0:T(8,128)(2,1)}, u32[]{:S(2)}) copy-start(bf16[1,192,2048]{2,1,0:T(8,128)(2,1)} %copy-done.13) | copy-start | bytes 2359300
  (9 other events, 9.7 us)
Sparse Core Ops, SparseCore 0:
  16.5 52.0 all-gather.8
  70.8 57.1 all-gather.12
  170.5 37.4 all-gather.10
  210.1 36.8 all-gather.14
  248.3 36.8 all-gather.16
  286.6 36.8 all-gather.18
  325.0 36.7 all-gather.20
  364.8 38.4 reduce-scatter.10
  406.1 38.1 reduce-scatter.12
  454.6 38.6 reduce-scatter.8
  521.4 28.9 reduce-scatter.16
  553.1 30.6 reduce-scatter.14
  613.2 34.2 reduce-scatter.18
  678.8 28.8 all-gather.22
  710.4 161.2 reduce-scatter.20
  874.4 88.3 reduce-scatter.22
